TPU v7x, 128 devices: a whole 4x4x4 slice. The times are simulated.
128 devices in a mesh: expert: 64 (over z, y, x_lo, core), dp: 2 (over x_hi).
Axes of the slice: x: 4 (x_hi: 2, x_lo: 2; x = x_hi * 2 + x_lo), y: 4, z: 4, core: 2. Of those that a mesh axis runs over, the one named last changes fastest.
Arguments:
- tokens: bfloat16 [16384, 2880], P(('expert', 'dp')), may hold values from -6 to 6
- cotangent: bfloat16 [16384, 2880], P(('expert', 'dp')), may hold values from -3 to 3
- expert_ids: int32 [16384, 4], P(('expert', 'dp')), may hold values from 0 to 63, as said below
- slots: int32 [16384, 4], P(('expert', 'dp')), may hold values from -1 to 5, as said below
- probs: float32 [16384, 4], P(('expert', 'dp')), may hold values from 0.1 to 0.6
- w_gate: bfloat16 [64, 2880, 1440], P('expert', None, 'dp'), may hold values from -0.109375 to 0.109375
- w_up: bfloat16 [64, 2880, 1440], P('expert', None, 'dp'), may hold values from -0.109375 to 0.109375
- w_down: bfloat16 [64, 2880, 1440], P('expert', None, 'dp'), may hold values from -0.15625 to 0.15625
Outputs:
- input_grad: bfloat16 [16384, 2880], P(('expert', 'dp'))
- prob_grad: float32 [16384, 4], P(('expert', 'dp'))
- grad_gate: bfloat16 [64, 2880, 1440], P('expert', None, 'dp')
- grad_up: bfloat16 [64, 2880, 1440], P('expert', None, 'dp')
- grad_down: bfloat16 [64, 2880, 1440], P('expert', None, 'dp')
Inputs may be any that keep to these rules, and one draw needn't show every extreme that they name: `expert_ids`: each row names 4 different experts. Within the 128 tokens of one device, the choices of one expert, taken in order of tokens and then of k, hold 0, 1, 2 and so on up to 5, and -1 after that; in every draw some expert fills all 6 slots from every device.
All inputs are finite; a program needn't handle non-finite values.
Results may differ from a plain program's by a relative error of at most 0.018.
Values may be sent and summed in bfloat16 or wider, within the bound.
A program may use at most 192 MiB of HBM per device.

v0:
```python
import jax
import jax.numpy as jnp
from jax import lax
from jax.sharding import PartitionSpec as P

ALPHA = 1.702


def split_up(shard, dim, size):
    lengths = shard.shape
    blocks = shard.reshape(*lengths[:dim], size, lengths[dim] // size, *lengths[dim + 1 :])
    return jnp.moveaxis(blocks, dim, 0)


def sum_at_owner(shard, axis, dim):
    blocks = split_up(shard, dim, lax.axis_size(axis))
    arrived = lax.all_to_all(blocks, axis, split_axis=0, concat_axis=0, tiled=True)
    return arrived.astype(jnp.float32).sum(axis=0)


def body(tokens, cotangent, expert_ids, slots, probs, w_gate, w_up, w_down):
    experts = lax.axis_size("expert")
    tok_rows = tokens.shape[0]
    width = tokens.shape[1]
    top_count = expert_ids.shape[1]
    capacity = max(2, 3 * tok_rows * top_count // (4 * experts))
    slot_total = experts * capacity
    kept = slots >= 0
    position = jnp.where(kept, expert_ids * capacity + slots, slot_total)
    owners = jnp.broadcast_to(jnp.arange(tok_rows, dtype=jnp.int32)[:, None], expert_ids.shape)
    slot_owner = (
        jnp.full((slot_total,), -1, jnp.int32)
        .at[position.reshape(-1)]
        .set(owners.reshape(-1), mode="drop")
    )
    slot_prob = (
        jnp.zeros((slot_total,), jnp.float32)
        .at[position.reshape(-1)]
        .set(probs.reshape(-1), mode="drop")
    )
    present = slot_owner >= 0
    source = jnp.maximum(slot_owner, 0)
    lookup = jnp.where(kept, expert_ids * capacity + slots, 0)
    zero_bf = jnp.zeros((), jnp.bfloat16)
    outgoing = jnp.where(present[:, None], tokens[source], zero_bf)
    arrived = lax.all_to_all(
        outgoing.reshape(experts, capacity, width),
        "expert",
        split_axis=0,
        concat_axis=0,
        tiled=True,
    )
    local_rows = arrived.reshape(slot_total, width)
    pair_rows = lax.all_gather(local_rows, "dp", axis=0, tiled=True)
    gate_w = w_gate[0]
    up_w = w_up[0]
    down_w = w_down[0]
    gate_pre = jnp.dot(pair_rows, gate_w, preferred_element_type=jnp.float32)
    up_pre = jnp.dot(pair_rows, up_w, preferred_element_type=jnp.float32)
    sigmoid_val = jax.nn.sigmoid(ALPHA * gate_pre)
    glu_value = gate_pre * sigmoid_val
    hidden = ((up_pre + 1.0) * glu_value).astype(jnp.bfloat16)
    contract_units = (((1,), (1,)), ((), ()))
    contract_rows = (((0,), (0,)), ((), ()))
    own_out = sum_at_owner(
        lax.dot_general(hidden, down_w, contract_units, preferred_element_type=jnp.float32).astype(
            jnp.bfloat16
        ),
        "dp",
        0,
    ).astype(jnp.bfloat16)
    plain_send = jnp.where(present[:, None], cotangent[source], zero_bf)
    plain_rows, prob_rows = (
        lax.all_to_all(
            plain_send.reshape(experts, capacity, width),
            "expert",
            split_axis=0,
            concat_axis=0,
            tiled=True,
        ),
        lax.all_to_all(
            slot_prob.reshape(experts, capacity).astype(jnp.bfloat16),
            "expert",
            split_axis=0,
            concat_axis=0,
            tiled=True,
        ).astype(jnp.float32),
    )
    plain_rows = plain_rows.reshape(slot_total, width)
    prob_rows = prob_rows.reshape(slot_total)
    slot_grad = jnp.einsum("rd,rd->r", plain_rows, own_out, preferred_element_type=jnp.float32)
    weighted = (prob_rows[:, None] * plain_rows.astype(jnp.float32)).astype(jnp.bfloat16)
    pair_cot = lax.all_gather(weighted, "dp", axis=0, tiled=True)
    hidden_grad = jnp.dot(pair_cot, down_w, preferred_element_type=jnp.float32)
    up_grad = (hidden_grad * glu_value).astype(jnp.bfloat16)
    gate_grad = (
        hidden_grad
        * (up_pre + 1.0)
        * (sigmoid_val + ALPHA * gate_pre * sigmoid_val * (1.0 - sigmoid_val))
    ).astype(jnp.bfloat16)
    grad_down = lax.dot_general(
        pair_cot, hidden, contract_rows, preferred_element_type=jnp.float32
    ).astype(jnp.bfloat16)
    grad_gate = lax.dot_general(
        pair_rows, gate_grad, contract_rows, preferred_element_type=jnp.float32
    ).astype(jnp.bfloat16)
    grad_up = lax.dot_general(
        pair_rows, up_grad, contract_rows, preferred_element_type=jnp.float32
    ).astype(jnp.bfloat16)
    result = lax.dot_general(gate_grad, gate_w, contract_units, preferred_element_type=jnp.float32)
    own_input = sum_at_owner(
        (
            result
            + lax.dot_general(up_grad, up_w, contract_units, preferred_element_type=jnp.float32)
        ).astype(jnp.bfloat16),
        "dp",
        0,
    ).astype(jnp.bfloat16)
    back_rows, back_prob = (
        lax.all_to_all(
            own_input.reshape(experts, capacity, width),
            "expert",
            split_axis=0,
            concat_axis=0,
            tiled=True,
        ),
        lax.all_to_all(
            slot_grad.reshape(experts, capacity).astype(jnp.bfloat16),
            "expert",
            split_axis=0,
            concat_axis=0,
            tiled=True,
        ).astype(jnp.float32),
    )
    back_rows = back_rows.reshape(slot_total, width)
    prob_grad = jnp.where(kept, back_prob.reshape(slot_total)[lookup], jnp.float32(0.0))
    picked_grad = back_rows[lookup]
    masked = jnp.where(kept[:, :, None], picked_grad, zero_bf)
    input_grad = jnp.sum(masked, axis=1, dtype=jnp.float32).astype(jnp.bfloat16)
    return (input_grad, prob_grad, grad_gate[None], grad_up[None], grad_down[None])


def solution(mesh):
    return jax.shard_map(
        body,
        mesh=mesh,
        in_specs=(
            P(("expert", "dp"), None),
            P(("expert", "dp"), None),
            P(("expert", "dp"), None),
            P(("expert", "dp"), None),
            P(("expert", "dp"), None),
            P("expert", None, "dp"),
            P("expert", None, "dp"),
            P("expert", None, "dp"),
        ),
        out_specs=(
            P(("expert", "dp"), None),
            P(("expert", "dp"), None),
            P("expert", None, "dp"),
            P("expert", None, "dp"),
            P("expert", None, "dp"),
        ),
        check_vma=False,
    )
```

profile of v0, /device:TPU:0, one launch (start us, length us, event | category | flops | bytes accessed | tf_op | source)
XLA Modules:
  0.0 474.6 jit_solution(521120281229968658)
XLA Ops:
  25.7 4.4 gather.19
  34.3 49.2 %all_to_all.37 = bf16[64,6,2880]{2,1,0:T(8,128)(2,1)S(1)} all-to-all(bf16[64,6,2880]{2,1,0:T(8,128)(2,1)S(1)} %get-tuple-element.25), channel_id=1, replica_groups=mesh['expert'=64,'dp'=2] {'expert'}, dimensions={0} | all-to-all | bytes 4423680 | tf_op jit(solution)/shard_map/all_to_all | solution.py:46
  89.1 12.4 %all_to_all.38 = bf16[64,1,6]{2,1,0:T(2,128)(2,1)S(1)} all-to-all(bf16[64,1,6]{2,1,0:T(2,128)(2,1)S(1)} %convert_element_type.99), channel_id=1, replica_groups=mesh['expert'=64,'dp'=2] {'expert'}, dimensions={0} | all-to-all | bytes 1536 | tf_op jit(solution)/shard_map/all_to_all | solution.py:81
  101.5 5.6 %all-to-all-start.1 = ((bf16[64,6,2880]{2,1,0:T(8,128)(2,1)}), bf16[64,6,2880]{2,1,0:T(8,128)(2,1)}, u32[]{:S(2)}, u32[]{:S(2)}) async-start(bf16[64,6,2880]{2,1,0:T(8,128)(2,1)} %get-tuple-element.26), calls=%async_computation.1 | async-start | bytes 6029312 | tf_op jit(solution)/shard_map/all_to_all | solution.py:74
  107.6 69.7 %all-to-all-done.1 = bf16[64,6,2880]{2,1,0:T(8,128)(2,1)} async-done(((bf16[64,6,2880]{2,1,0:T(8,128)(2,1)}), bf16[64,6,2880]{2,1,0:T(8,128)(2,1)}, u32[]{:S(2)}, u32[]{:S(2)}) %all-to-all-start.1) | async-done | bytes 2211872 | tf_op jit(solution)/shard_map/all_to_all | solution.py:74
  182.8 8.5 %fusion.5 = f32[768,720]{0,1:T(8,128)} fusion(bf16[768,2880]{1,0:T(8,128)(2,1)} %all-gather.5.cloned.1.call-done, bf16[1,2880,720]{1,2,0:T(8,128)(2,1)} %param.13), kind=kOutput, calls=%fused_computation.20 | convolution fusion | flops 3185049600 | bytes 10782720 | tf_op jit(solution)/shard_map/dot_general | solution.py:58
  191.3 54.8 %all-gather.3.cloned.1.call-done = bf16[768,2880]{1,0:T(8,128)(2,1)} async-done(((bf16[384,2880]{1,0:T(8,128)(2,1)}), bf16[768,2880]{1,0:T(8,128)(2,1)}) %all-gather.3.cloned.1.call-update) | async-done | bytes 4423696 | tf_op jit(solution)/shard_map/all_gather | solution.py:93
  246.1 6.9 %fusion.11 = f32[768,720]{0,1:T(8,128)S(1)} fusion(bf16[768,2880]{1,0:T(8,128)(2,1)} %all-gather.3.cloned.1.call-done, bf16[1,2880,720]{1,2,0:T(8,128)(2,1)} %param.15), kind=kOutput, calls=%fused_computation.26 | convolution fusion | flops 3185049600 | bytes 10782720 | tf_op jit(solution)/shard_map/dot_general | solution.py:94
  253.0 8.0 %multiply_convert_fusion.1 = (bf16[768,720]{0,1:T(8,128)(2,1)S(1)}, bf16[768,720]{0,1:T(8,128)(2,1)}, bf16[768,720]{0,1:T(8,128)(2,1)}) fusion(f32[768,720]{0,1:T(8,128)S(1)} %copy-done.6, f32[768,720]{0,1:T(8,128)S(1)} %fusion.11, bf16[768,2880]{1,0:T(8,128)(2,1)S(1)} %copy-done.2, bf16[1,2880,720]{1,2,0:T(8,128)(2,1)} %param.14), kind=kOutput, calls=%fused_computation.31 | convolution fusion | flops 3194449920 | bytes 16312320 | tf_op jit(solution)/shard_map/dot_general | solution.py:59
  267.8 5.9 %all-to-all-start.5 = ((bf16[2,384,2880]{1,2,0:T(8,128)(2,1)}), bf16[2,384,2880]{1,2,0:T(8,128)(2,1)}, u32[]{:S(2)}, u32[]{:S(2)}) async-start(bf16[2,384,2880]{1,2,0:T(8,128)(2,1)} %bitcast.47), calls=%async_computation.5 | async-start | bytes 8847360 | tf_op jit(solution)/shard_map/all_to_all | solution.py:17
  273.6 6.6 %fusion.3 = f32[768,2880]{0,1:T(8,128)S(1)} fusion(bf16[768,720]{0,1:T(8,128)(2,1)} %get-tuple-element.23, bf16[1,2880,720]{1,2,0:T(8,128)(2,1)} %param.13), kind=kOutput, calls=%fused_computation.18 | convolution fusion | flops 3185049600 | bytes 14100480 | tf_op jit(solution)/shard_map/dot_general | solution.py:110
  280.3 6.3 %add_convert_fusion = bf16[768,2880]{0,1:T(8,128)(2,1)S(1)} fusion(f32[768,2880]{0,1:T(8,128)S(1)} %fusion.3, bf16[768,720]{0,1:T(8,128)(2,1)S(1)} %copy-done.3, bf16[1,2880,720]{1,2,0:T(8,128)(2,1)} %param.14), kind=kOutput, calls=%fused_computation.6 | convolution fusion | flops 3189473280 | bytes 18524160 | tf_op jit(solution)/shard_map/dot_general | solution.py:114
  289.1 35.9 %all-to-all-done.5 = bf16[2,384,2880]{1,2,0:T(8,128)(2,1)} async-done(((bf16[2,384,2880]{1,2,0:T(8,128)(2,1)}), bf16[2,384,2880]{1,2,0:T(8,128)(2,1)}, u32[]{:S(2)}, u32[]{:S(2)}) %all-to-all-start.5) | async-done | bytes 4423712 | tf_op jit(solution)/shard_map/all_to_all | solution.py:17
  325.1 5.6 %all-to-all-start.3 = ((bf16[2,384,2880]{1,2,0:T(8,128)(2,1)}), bf16[2,384,2880]{1,2,0:T(8,128)(2,1)}, u32[]{:S(2)}, u32[]{:S(2)}) async-start(bf16[2,384,2880]{1,2,0:T(8,128)(2,1)} %bitcast.46), calls=%async_computation.3 | async-start | bytes 8847360 | tf_op jit(solution)/shard_map/all_to_all | solution.py:17
  334.1 4.6 reduce_sum.38
  342.3 39.0 %all-to-all-done.3 = bf16[2,384,2880]{1,2,0:T(8,128)(2,1)} async-done(((bf16[2,384,2880]{1,2,0:T(8,128)(2,1)}), bf16[2,384,2880]{1,2,0:T(8,128)(2,1)}, u32[]{:S(2)}, u32[]{:S(2)}) %all-to-all-start.3) | async-done | bytes 4423712 | tf_op jit(solution)/shard_map/all_to_all | solution.py:17
  381.3 7.9 %all-to-all-start.6 = ((bf16[64,1,6]{2,1,0:T(2,128)(2,1)}), bf16[64,1,6]{2,1,0:T(2,128)(2,1)S(1)}, u32[]{:S(2)}, u32[]{:S(2)}) async-start(bf16[64,1,6]{2,1,0:T(2,128)(2,1)} %convert_element_type.100), calls=%async_computation.6 | async-start | bytes 65536 | tf_op jit(solution)/shard_map/all_to_all | solution.py:127
  389.4 5.1 %reduce_sum.36 = bf16[384,2880]{0,1:T(8,128)(2,1)} reduce(bf16[2,384,2880]{1,2,0:T(8,128)(2,1)} %all-to-all-done.3, bf16[]{:T(256)} %constant.13.clone.1), dimensions={0}, to_apply=%region_2.3 | reduce | flops 1105920 | bytes 6635522 | tf_op jit(solution)/shard_map/reduce_sum | solution.py:18
  399.9 9.2 %all-to-all-start.4 = ((bf16[64,6,2880]{2,1,0:T(8,128)(2,1)}), bf16[64,6,2880]{2,1,0:T(8,128)(2,1)}, u32[]{:S(2)}, u32[]{:S(2)}) async-start(bf16[64,6,2880]{2,1,0:T(8,128)(2,1)} %reshape.126), calls=%async_computation.4 | async-start | bytes 6029312 | tf_op jit(solution)/shard_map/all_to_all | solution.py:120
  409.1 7.6 %fusion.2 = bf16[1,2880,720]{1,2,0:T(8,128)(2,1)} fusion(bf16[768,720]{0,1:T(8,128)(2,1)S(1)} %copy-done.8, bf16[768,2880]{1,0:T(8,128)(2,1)} %all-gather.3.cloned.1.call-done), kind=kOutput, calls=%fused_computation.17 | convolution fusion | flops 3187123200 | bytes 9676800 | tf_op jit(solution)/shard_map/dot_general | solution.py:101
  416.7 5.1 %fusion = bf16[1,2880,720]{1,2,0:T(8,128)(2,1)} fusion(bf16[768,720]{0,1:T(8,128)(2,1)S(1)} %copy-done.5, bf16[768,2880]{1,0:T(8,128)(2,1)S(1)} %bitcast.53), kind=kOutput, calls=%fused_computation.15 | convolution fusion | flops 3187123200 | bytes 9676800 | tf_op jit(solution)/shard_map/dot_general | solution.py:104
  421.9 5.1 %fusion.1 = bf16[1,2880,720]{1,2,0:T(8,128)(2,1)} fusion(bf16[768,720]{0,1:T(8,128)(2,1)S(1)} %copy-done.4, bf16[768,2880]{1,0:T(8,128)(2,1)S(1)} %bitcast.53), kind=kOutput, calls=%fused_computation.16 | convolution fusion | flops 3187123200 | bytes 9676800 | tf_op jit(solution)/shard_map/dot_general | solution.py:107
  431.5 17.6 %all-to-all-done.4 = bf16[64,6,2880]{2,1,0:T(8,128)(2,1)} async-done(((bf16[64,6,2880]{2,1,0:T(8,128)(2,1)}), bf16[64,6,2880]{2,1,0:T(8,128)(2,1)}, u32[]{:S(2)}, u32[]{:S(2)}) %all-to-all-start.4) | async-done | bytes 2211872 | tf_op jit(solution)/shard_map/all_to_all | solution.py:120
  456.2 4.7 reshape.148
  (84 shorter events, 74.0 us)
Async XLA Ops:
  7.2 175.6 %all-gather.5.cloned.1.call-start = ((), (), s32[]{:S(2)}) async-start(), calls=%async_computation.8 | async-start | bytes 6782976 | tf_op jit(solution)/shard_map/all_gather | solution.py:54
  25.7 4.5 copy-start
  83.6 2.7 copy-start.1
  101.5 75.8 %all-to-all-start.1 = ((bf16[64,6,2880]{2,1,0:T(8,128)(2,1)}), bf16[64,6,2880]{2,1,0:T(8,128)(2,1)}, u32[]{:S(2)}, u32[]{:S(2)}) async-start(bf16[64,6,2880]{2,1,0:T(8,128)(2,1)} %get-tuple-element.26), calls=%async_computation.1 | async-start | bytes 6029312 | tf_op jit(solution)/shard_map/all_to_all | solution.py:74
  107.1 139.0 %all-gather.3.cloned.1.call-start = ((), (), s32[]{:S(2)}) async-start(), calls=%async_computation.7 | async-start | bytes 6782976 | tf_op jit(solution)/shard_map/all_gather | solution.py:93
  246.1 6.9 %copy-start.2 = (bf16[768,2880]{1,0:T(8,128)(2,1)S(1)}, bf16[768,2880]{1,0:T(8,128)(2,1)}, u32[]{:S(2)}) copy-start(bf16[768,2880]{1,0:T(8,128)(2,1)} %all-gather.5.cloned.1.call-done) | copy-start | bytes 13271044
  246.1 6.9 %copy-start.6 = (f32[768,720]{0,1:T(8,128)S(1)}, f32[768,720]{0,1:T(8,128)}, u32[]{:S(2)}) copy-start(f32[768,720]{0,1:T(8,128)} %fusion.5) | copy-start | bytes 6635524
  246.1 14.9 %slice-start.2 = ((s8[4239360]{0:T(1024)(128)(4,1)}), s8[4194304]{0:T(1024)(128)(4,1)S(1)}, s32[]{:S(2)}) async-start(s8[4239360]{0:T(1024)(128)(4,1)} %bitcast.54), calls=%async_computation.11 | async-start | bytes 8388608
  253.0 8.0 %slice-start.3 = ((s8[4239360]{0:T(1024)(128)(4,1)}), s8[45056]{0:T(1024)(128)(4,1)S(1)}, s32[]{:S(2)}) async-start(s8[4239360]{0:T(1024)(128)(4,1)} %bitcast.54), calls=%async_computation.12 | async-start | bytes 90112
  261.0 4.3 copy-start.7
  267.8 57.3 %all-to-all-start.5 = ((bf16[2,384,2880]{1,2,0:T(8,128)(2,1)}), bf16[2,384,2880]{1,2,0:T(8,128)(2,1)}, u32[]{:S(2)}, u32[]{:S(2)}) async-start(bf16[2,384,2880]{1,2,0:T(8,128)(2,1)} %bitcast.47), calls=%async_computation.5 | async-start | bytes 8847360 | tf_op jit(solution)/shard_map/all_to_all | solution.py:17
  273.6 6.6 %copy-start.3 = (bf16[768,720]{0,1:T(8,128)(2,1)S(1)}, bf16[768,720]{0,1:T(8,128)(2,1)}, u32[]{:S(2)}) copy-start(bf16[768,720]{0,1:T(8,128)(2,1)} %get-tuple-element.24) | copy-start | bytes 3317764
  325.1 56.2 %all-to-all-start.3 = ((bf16[2,384,2880]{1,2,0:T(8,128)(2,1)}), bf16[2,384,2880]{1,2,0:T(8,128)(2,1)}, u32[]{:S(2)}, u32[]{:S(2)}) async-start(bf16[2,384,2880]{1,2,0:T(8,128)(2,1)} %bitcast.46), calls=%async_computation.3 | async-start | bytes 8847360 | tf_op jit(solution)/shard_map/all_to_all | solution.py:17
  381.3 18.6 %all-to-all-start.6 = ((bf16[64,1,6]{2,1,0:T(2,128)(2,1)}), bf16[64,1,6]{2,1,0:T(2,128)(2,1)S(1)}, u32[]{:S(2)}, u32[]{:S(2)}) async-start(bf16[64,1,6]{2,1,0:T(2,128)(2,1)} %convert_element_type.100), calls=%async_computation.6 | async-start | bytes 65536 | tf_op jit(solution)/shard_map/all_to_all | solution.py:127
  399.9 9.2 %copy-start.8 = (bf16[768,720]{0,1:T(8,128)(2,1)S(1)}, bf16[768,720]{0,1:T(8,128)(2,1)}, u32[]{:S(2)}) copy-start(bf16[768,720]{0,1:T(8,128)(2,1)} %copy-done.7) | copy-start | bytes 3317764
  399.9 16.8 %slice-start = ((s8[4521984]{0:T(1024)(128)(4,1)}), s8[327680]{0:T(1024)(128)(4,1)S(1)}, s32[]{:S(2)}) async-start(s8[4521984]{0:T(1024)(128)(4,1)} %bitcast.52), calls=%async_computation.9 | async-start | bytes 655360
  399.9 49.2 %all-to-all-start.4 = ((bf16[64,6,2880]{2,1,0:T(8,128)(2,1)}), bf16[64,6,2880]{2,1,0:T(8,128)(2,1)}, u32[]{:S(2)}, u32[]{:S(2)}) async-start(bf16[64,6,2880]{2,1,0:T(8,128)(2,1)} %reshape.126), calls=%async_computation.4 | async-start | bytes 6029312 | tf_op jit(solution)/shard_map/all_to_all | solution.py:120
  409.1 7.6 %slice-start.1 = ((s8[4521984]{0:T(1024)(128)(4,1)}), s8[4194304]{0:T(1024)(128)(4,1)S(1)}, s32[]{:S(2)}) async-start(s8[4521984]{0:T(1024)(128)(4,1)} %bitcast.52), calls=%async_computation.10 | async-start | bytes 8388608
  409.1 7.6 %copy-start.5 = (bf16[768,720]{0,1:T(8,128)(2,1)S(1)}, bf16[768,720]{0,1:T(8,128)(2,1)}, u32[]{:S(2)}) copy-start(bf16[768,720]{0,1:T(8,128)(2,1)} %get-tuple-element.23) | copy-start | bytes 3317764
  416.7 5.1 %copy-start.4 = (bf16[768,720]{0,1:T(8,128)(2,1)S(1)}, bf16[768,720]{0,1:T(8,128)(2,1)}, u32[]{:S(2)}) copy-start(bf16[768,720]{0,1:T(8,128)(2,1)} %get-tuple-element.24) | copy-start | bytes 3317764
Sparse Core Ops, SparseCore 0:
  86.4 93.4 all-gather.4
  182.8 63.1 all-gather.2
where the time goes:
time: 484 us; the launch traced here: 475 us
  waiting for transfers between devices  217 us (45%)
  local copies, waits for them, and re-layouts  63.1 us (13%)
  blocking collectives  61.6 us (13%)
  matrix products  58.4 us (12%)
  starting transfers between devices  34.4 us (7%)
  other arithmetic  25.1 us (5%)
  between operations  14.8 us (3%)
    all_to_all x2, waiting for transfers between devices, sum_at_owner(): lax.all_to_all(blocks, axis, split_axis=0, concat_axis=0, tiled=True)  74.9 us
    all_to_all x1, waiting for transfers between devices, body(): lax.all_to_all(plain_send.reshape(experts, capacity, width), 'expert', sp...  69.7 us
    all_gather x1, waiting for transfers between devices, body(): pair_cot = lax.all_gather(weighted, 'dp', axis=0, tiled=True)  54.8 us
    all_to_all x1, blocking collectives, body(): lax.all_to_all(outgoing.reshape(experts, capacity, width), 'expert', spli...  49.2 us
    all_to_all x1, waiting for transfers between devices, body(): lax.all_to_all(own_input.reshape(experts, capacity, width), 'expert', spl...  17.6 us
    all_to_all x1, blocking collectives, body(): lax.all_to_all(slot_prob.reshape(experts, capacity).astype(jnp.bfloat16),...  12.4 us
    all_to_all x2, starting transfers between devices, sum_at_owner(): lax.all_to_all(blocks, axis, split_axis=0, concat_axis=0, tiled=True)  11.5 us
  transfers between devices with their start and end apart: 7, of which 5 were waited for; matrix products, arithmetic and copies ran while one was open for 16% of the time, Pallas kernels for 0%

commit v1 on v0

v1 whole, which is shorter than its diff:
```python
import functools

import jax
import jax.numpy as jnp
from jax import lax
from jax.experimental import pallas as pl
from jax.experimental.pallas import tpu as pltpu
from jax.sharding import PartitionSpec as P

ALPHA = 1.702
BF = jnp.bfloat16
F32 = jnp.float32
CAP = 6
MROWS = 8
MAIN = 2304
CHUNK = 640


def dot(a, b):
    return jnp.dot(a, b, preferred_element_type=F32)


def dot_nt(a, b):
    return lax.dot_general(a, b, (((1,), (1,)), ((), ())), preferred_element_type=F32)


def iota(shape, dim):
    return lax.broadcasted_iota(jnp.int32, shape, dim)


def pack_kernel(expert_ref, slot_ref, prob_ref, tok_ref, cot_ref, rows_ref, wt_ref, rem_ref):
    toks = tok_ref.shape[0]
    rest = tok_ref.shape[1] - MAIN
    total = rows_ref.shape[0]
    row = iota((total, toks), 0)
    zero = jnp.zeros((total, toks), F32)
    one, par, orem, prem = zero, zero, [zero] * 3, [zero] * 3
    for k in range(expert_ref.shape[0]):
        expert, slot, prob = expert_ref[k : k + 1, :], slot_ref[k : k + 1, :], prob_ref[k : k + 1, :]
        kept = slot >= 0
        hit = row == jnp.where(kept, expert * MROWS + slot, -1)
        one = jnp.where(hit, 1.0, one)
        par = jnp.where(hit, prob, par)
        high = jnp.where(slot >= 3, 1, 0)
        place = expert * MROWS + CAP + high
        for j in range(3):
            hit = row == jnp.where(kept & (slot - 3 * high == j), place, -1)
            orem[j] = jnp.where(hit, 1.0, orem[j])
            prem[j] = jnp.where(hit, prob, prem[j])
    rem_ref[...] = jnp.zeros_like(rem_ref)
    for src, dst, main, extra in ((tok_ref, rows_ref, one, orem), (cot_ref, wt_ref, par, prem)):
        rem_ref[:, :rest] = src[:, MAIN:]
        main = main.astype(BF)
        for j in range(3):
            cols = slice(j * CHUNK, (j + 1) * CHUNK)
            part = dot(main, src[:, cols]) + dot(extra[j].astype(BF), rem_ref[...])
            dst[:, cols] = part.astype(BF)
        cols = slice(3 * CHUNK, MAIN)
        dst[:, cols] = dot(main, src[:, cols]).astype(BF)


def pack(expert_t, slot_t, prob_t, tokens, cotangent, experts):
    shape = jax.ShapeDtypeStruct((experts * MROWS, MAIN), BF)
    return pl.pallas_call(
        pack_kernel,
        out_shape=(shape, shape),
        scratch_shapes=[pltpu.VMEM((tokens.shape[0], CHUNK), BF)],
        compiler_params=pltpu.CompilerParams(vmem_limit_bytes=40 * 2**20),
    )(expert_t, slot_t, prob_t, tokens, cotangent)


def picks(out_rows, in_rows, wide):
    if wide:
        q, o = iota((out_rows, in_rows), 0), iota((out_rows, in_rows), 1)
    else:
        o, q = iota((out_rows, in_rows), 0), iota((out_rows, in_rows), 1)
    message = o // CAP
    slot = o - CAP * message
    base = q - MROWS * message
    high = jnp.where(slot >= 3, 1, 0)
    main = jnp.where(base == slot, 1.0, 0.0).astype(BF)
    last = base == CAP + high
    rem = [jnp.where(last & (slot - 3 * high == j), 1.0, 0.0).astype(BF) for j in range(3)]
    return main, rem, jnp.where(last, 1.0, 0.0).astype(BF)


def unpack_into(src, dst):
    main, rem, _ = picks(dst.shape[0], src.shape[0], False)
    rest = dst.shape[1] - MAIN
    dst[:, :MAIN] = dot(main, src[:, :MAIN]).astype(BF)
    part = dot(rem[0], src[:, :rest])
    for j in (1, 2):
        part = part + dot(rem[j], src[:, j * CHUNK : j * CHUNK + rest])
    dst[:, MAIN:] = part.astype(BF)


def forward_kernel(msg_ref, gate_ref, up_ref, rows_ref, hidden_ref, glu_ref, slope_ref):
    unpack_into(msg_ref, rows_ref)
    gate = dot(rows_ref[...], gate_ref[...])
    up = dot(rows_ref[...], up_ref[...]) + 1.0
    sig = jax.nn.sigmoid(ALPHA * gate)
    glu = gate * sig
    hidden_ref[...] = (up * glu).astype(BF)
    glu_ref[...] = glu
    slope_ref[...] = up * (sig + ALPHA * glu * (1.0 - sig))


def forward(msgs, gate_w, up_w, tile):
    width, units = gate_w.shape
    groups = msgs.shape[0] // MROWS
    steps = groups * CAP // tile
    wide = tile // CAP * MROWS
    block = lambda cols: pl.BlockSpec((tile, cols), lambda i: (i, 0))
    whole = pl.BlockSpec((width, units), lambda i: (0, 0))
    rows = groups * CAP
    return pl.pallas_call(
        forward_kernel,
        grid=(steps,),
        in_specs=[pl.BlockSpec((wide, MAIN), lambda i: (i, 0)), whole, whole],
        out_specs=[block(width), block(units), block(units), block(units)],
        out_shape=[
            jax.ShapeDtypeStruct((rows, width), BF),
            jax.ShapeDtypeStruct((rows, units), BF),
            jax.ShapeDtypeStruct((rows, units), F32),
            jax.ShapeDtypeStruct((rows, units), F32),
        ],
        compiler_params=pltpu.CompilerParams(vmem_limit_bytes=60 * 2**20),
        cost_estimate=pl.CostEstimate(flops=4 * rows * width * units, bytes_accessed=20 * 2**20, transcendentals=0),
    )(msgs, gate_w, up_w)


def backward_kernel(
    msg_ref, gate_ref, up_ref, down_ref, hidden_ref, glu_ref, slope_ref, wt_ref, gg_ref, ug_ref, out_ref, full_ref
):
    tile = wt_ref.shape[0]
    width = wt_ref.shape[1]
    unpack_into(msg_ref, wt_ref)
    hgrad = dot(wt_ref[...], down_ref[...])
    share = jnp.sum(hgrad * hidden_ref[...].astype(F32), axis=1, keepdims=True)
    ug_ref[...] = (hgrad * glu_ref[...]).astype(BF)
    gg_ref[...] = (hgrad * slope_ref[...]).astype(BF)
    full_ref[:, width:] = jnp.zeros((tile, full_ref.shape[1] - width), BF)
    full_ref[:, :width] = (dot_nt(gg_ref[...], gate_ref[...]) + dot_nt(ug_ref[...], up_ref[...])).astype(BF)
    main, rem, last = picks(out_ref.shape[0], tile, True)
    tail = full_ref[:, MAIN : MAIN + CHUNK]
    for j in range(3):
        cols = slice(j * CHUNK, (j + 1) * CHUNK)
        out_ref[:, cols] = (dot(main, full_ref[:, cols]) + dot(rem[j], tail)).astype(BF)
    spare = MAIN - 3 * CHUNK
    lane = iota((tile, spare), 1)
    row = iota((tile, spare), 0)
    head = share.astype(BF).astype(F32)
    spot = 2 * ((row % CAP) % 3)
    pair = jnp.where(lane == spot, head, jnp.where(lane == spot + 1, share - head, 0.0)).astype(BF)
    cols = slice(3 * CHUNK, MAIN)
    out_ref[:, cols] = (dot(main, full_ref[:, cols]) + dot(last, pair)).astype(BF)


def backward(msgs, gate_w, up_w, down_w, hidden, glu, slope, tile):
    width, units = gate_w.shape
    rows = hidden.shape[0]
    wide = tile // CAP * MROWS
    block = lambda cols: pl.BlockSpec((tile, cols), lambda i: (i, 0))
    whole = pl.BlockSpec((width, units), lambda i: (0, 0))
    packed = pl.BlockSpec((wide, MAIN), lambda i: (i, 0))
    return pl.pallas_call(
        backward_kernel,
        grid=(rows // tile,),
        in_specs=[packed, whole, whole, whole, block(units), block(units), block(units)],
        out_specs=[block(width), block(units), block(units), packed],
        out_shape=[
            jax.ShapeDtypeStruct((rows, width), BF),
            jax.ShapeDtypeStruct((rows, units), BF),
            jax.ShapeDtypeStruct((rows, units), BF),
            jax.ShapeDtypeStruct(msgs.shape, BF),
        ],
        scratch_shapes=[pltpu.VMEM((tile, MAIN + CHUNK), BF)],
        compiler_params=pltpu.CompilerParams(vmem_limit_bytes=60 * 2**20),
        cost_estimate=pl.CostEstimate(flops=6 * rows * width * units, bytes_accessed=30 * 2**20, transcendentals=0),
    )(msgs, gate_w, up_w, down_w, hidden, glu, slope)


def combine_kernel(copies, expert_ref, slot_ref, prob_ref, back_ref, in_ref, prob_out_ref):
    toks, rest = in_ref.shape[0], in_ref.shape[1] - MAIN
    total = back_ref.shape[0]
    col = iota((toks, total), 1)
    message = col // MROWS
    place = col - message * MROWS
    holder = message // copies
    zero = jnp.zeros((toks, total), F32)
    main, rem = zero, [zero] * 3
    sums = []
    lane = iota((toks, 128), 1)
    shares = back_ref[:, 3 * CHUNK : 3 * CHUNK + 128]
    for k in range(expert_ref.shape[1]):
        expert, slot = expert_ref[:, k : k + 1], slot_ref[:, k : k + 1]
        kept = slot >= 0
        mine = holder == jnp.where(kept, expert, -1)
        high = jnp.where(slot >= 3, 1, 0)
        which = slot - 3 * high
        main = jnp.where(mine & (place == slot), 1.0, main)
        tail = mine & (place == CAP + high)
        for j in range(3):
            rem[j] = jnp.where(tail & (which == j), 1.0, rem[j])
        got = dot(jnp.where(tail, 1.0, 0.0).astype(BF), shares)
        got = jnp.where((lane == 2 * which) | (lane == 2 * which + 1), got, 0.0)
        sums.append(jnp.sum(got, axis=1, keepdims=True))
    in_ref[:, :MAIN] = dot(main.astype(BF), back_ref[...]).astype(BF)
    part = dot(rem[0].astype(BF), back_ref[:, :rest])
    for j in (1, 2):
        part = part + dot(rem[j].astype(BF), back_ref[:, j * CHUNK : j * CHUNK + rest])
    in_ref[:, MAIN:] = part.astype(BF)
    choice = iota(prob_ref.shape, 1)
    total_share = jnp.zeros(prob_ref.shape, F32)
    for k, value in enumerate(sums):
        total_share = jnp.where(choice == k, value, total_share)
    prob_out_ref[...] = jnp.where(slot_ref[...] >= 0, total_share / prob_ref[...], 0.0)


def combine(expert_ids, slots, probs, back, width, copies):
    return pl.pallas_call(
        functools.partial(combine_kernel, copies),
        out_shape=(
            jax.ShapeDtypeStruct((expert_ids.shape[0], width), BF),
            jax.ShapeDtypeStruct(probs.shape, F32),
        ),
        compiler_params=pltpu.CompilerParams(vmem_limit_bytes=40 * 2**20),
    )(expert_ids, slots, probs, back)


def body(tokens, cotangent, expert_ids, slots, probs, w_gate, w_up, w_down):
    experts = lax.axis_size("expert")
    copies = lax.axis_size("dp")
    devices = experts * copies
    width = tokens.shape[1]
    gate_w, up_w, down_w = w_gate[0], w_up[0], w_down[0]
    rounded = probs.astype(BF).astype(F32)
    rows_msg, wt_msg = pack(expert_ids.T, slots.T, rounded.T, tokens, cotangent, experts)

    def spread(msg):
        msg = jnp.broadcast_to(msg.reshape(experts, 1, MROWS, MAIN), (experts, copies, MROWS, MAIN))
        msg = msg.reshape(devices, MROWS, MAIN)
        return lax.all_to_all(msg, ("expert", "dp"), split_axis=0, concat_axis=0, tiled=True)

    rows_in = spread(rows_msg).reshape(devices * MROWS, MAIN)
    wt_in = spread(wt_msg).reshape(devices * MROWS, MAIN)
    rows, hidden, glu, slope = forward(rows_in, gate_w, up_w, 192)
    weighted, gate_grad, up_grad, packed = backward(wt_in, gate_w, up_w, down_w, hidden, glu, slope, 192)
    back = lax.all_to_all(
        packed.reshape(devices, MROWS, MAIN), ("expert", "dp"), split_axis=0, concat_axis=0, tiled=True
    ).reshape(devices * MROWS, MAIN)
    contract_rows = (((0,), (0,)), ((), ()))
    grad_down = lax.dot_general(weighted, hidden, contract_rows, preferred_element_type=F32).astype(BF)
    grad_gate = lax.dot_general(rows, gate_grad, contract_rows, preferred_element_type=F32).astype(BF)
    grad_up = lax.dot_general(rows, up_grad, contract_rows, preferred_element_type=F32).astype(BF)
    input_grad, prob_grad = combine(expert_ids, slots, rounded, back, width, copies)
    return input_grad, prob_grad, grad_gate[None], grad_up[None], grad_down[None]


def solution(mesh):
    token_spec = P(("expert", "dp"), None)
    weight_spec = P("expert", None, "dp")
    return jax.shard_map(
        body,
        mesh=mesh,
        in_specs=(token_spec,) * 5 + (weight_spec,) * 3,
        out_specs=(token_spec,) * 2 + (weight_spec,) * 3,
        check_vma=False,
    )
```

time: 484 us -> 245 us (0.51); the launches traced: 475 us -> 244 us
  waiting for transfers between devices: 217 us -> 58.8 us
  Pallas kernels: 0 us -> 52.5 us
  matrix products: 58.4 us -> 20.9 us
  local copies, waits for them, and re-layouts: 63.1 us -> 29.3 us
  other arithmetic: 25.1 us -> 0.7 us
  starting transfers between devices: 34.4 us -> 12.1 us
  between operations: 14.8 us -> 0.76 us
  blocking collectives: 61.6 us -> 69.4 us
    all_to_all x5 -> x2, waiting for transfers between devices: 162 us -> 58.8 us  [the longest x1 36.4 us: body(): lax.all_to_all(packed.reshape(devices, MROWS, MAIN), ('expert', 'dp'), sp...]
    all_gather x2 -> x0, waiting for transfers between devices: 54.8 us -> none  [the longest x1 54.8 us: body(): pair_cot = lax.all_gather(weighted, 'dp', axis=0, tiled=True)]
    pallas_call x0 -> x4, Pallas kernels: none -> 52.5 us  [the longest x1 29.9 us: backward(): pl.pallas_call(backward_kernel, grid=(rows // tile,), in_specs=[packed, w...]
    dot_general x9 -> x3, matrix products: 58.4 us -> 20.9 us  [the longest x1 7.85 us: body(): lax.dot_general(weighted, hidden, contract_rows, preferred_element_type=F32)]
    gather x9 -> x0, local copies, waits for them, and re-layouts: 27.7 us -> none  [the longest x2 8.38 us: body(): picked_grad = back_rows[lookup]]
    all_to_all x5 -> x2, starting transfers between devices: 34.2 us -> 12.1 us  [the longest x1 6.15 us: body(): lax.all_to_all(packed.reshape(devices, MROWS, MAIN), ('expert', 'dp'), sp...]
    unnamed x31 -> x27, local copies, waits for them, and re-layouts: 8.51 us -> 26.3 us
    reshape x9 -> x0, local copies, waits for them, and re-layouts: 17.2 us -> none  [the longest x2 5.05 us: split_up(): shard.reshape(*lengths[:dim], size, lengths[dim] // size, *lengths[dim +...]
  transfers between devices with their start and end apart: 7 -> 2, of which waited for: 5 -> 2; matrix products, arithmetic and copies ran while one was open for 16% -> 17% of each run, Pallas kernels for 0% -> 6%
where the time goes in v1:
time: 245 us; the launch traced here: 244 us
  blocking collectives  69.4 us (28%)
  waiting for transfers between devices  58.8 us (24%)
  Pallas kernels  52.5 us (21%)
  local copies, waits for them, and re-layouts  29.3 us (12%)
  matrix products  20.9 us (9%)
  starting transfers between devices  12.1 us (5%)
    all_to_all x1, blocking collectives, spread(): lax.all_to_all(msg, ('expert', 'dp'), split_axis=0, concat_axis=0, tiled=...  69.4 us
    all_to_all x1, waiting for transfers between devices, body(): lax.all_to_all(packed.reshape(devices, MROWS, MAIN), ('expert', 'dp'), sp...  36.4 us
    pallas_call x1, Pallas kernels, backward(): pl.pallas_call(backward_kernel, grid=(rows // tile,), in_specs=[packed, w...  29.9 us
    unnamed x27, local copies, waits for them, and re-layouts  26.3 us
    all_to_all x1, waiting for transfers between devices, spread(): lax.all_to_all(msg, ('expert', 'dp'), split_axis=0, concat_axis=0, tiled=...  22.4 us
    pallas_call x1, Pallas kernels, forward(): pl.pallas_call(forward_kernel, grid=(steps,), in_specs=[pl.BlockSpec((wid...  15.2 us
    dot_general x1, matrix products, body(): lax.dot_general(weighted, hidden, contract_rows, preferred_element_type=F32)  7.85 us
    dot_general x1, matrix products, body(): lax.dot_general(rows, up_grad, contract_rows, preferred_element_type=F32)  7.8 us
  transfers between devices with their start and end apart: 2, of which 2 were waited for; matrix products, arithmetic and copies ran while one was open for 17% of the time, Pallas kernels for 6%

profile of v1, /device:TPU:0, one launch (start us, length us, event | category | flops | bytes accessed | tf_op | source)
XLA Modules:
  0.0 244.5 jit_solution(5046318053836809136)
XLA Ops:
  0.6 0.7 convert_element_type.15
  1.5 1.5 copy.15.tok_ref
  3.0 1.5 copy.16.cot_ref
  4.5 0.7 copy-done
  5.2 0.7 copy-done.2
  5.8 2.7 %shard_map.119 = (bf16[512,2304]{1,0:T(8,128)(2,1)S(1)}, bf16[512,2304]{1,0:T(8,128)(2,1)S(1)}) custom-call(s32[4,128]{1,0:T(4,128)S(1)} %bitcast.29, s32[4,128]{1,0:T(4,128)S(1)} %bitcast.30, f32[4,128]{1,0:T(4,128)S(1)} %copy.14.prob_ref, bf16[128,2880]{1,0:T(8,128)(2,1)S(1)} %copy.15.tok_ref, bf16[128,2880]{1,0:T(8,128)(2,1)S(1)} %copy.16.cot_ref), custom_call_target="tpu_custom_call" | custom-call | tf_op jit(solution)/shard_map/pallas_call | solution.py:64
  8.5 0.3 broadcast_in_dim.26
  8.8 69.4 %all_to_all.15 = bf16[128,8,2304]{2,1,0:T(8,128)(2,1)} all-to-all(bf16[128,8,2304]{2,1,0:T(8,128)(2,1)S(1)} %bitcast.32), channel_id=1, replica_groups=mesh['expert'=64,'dp'=2] {'expert','dp'}, dimensions={0} | all-to-all | bytes 9437184 | tf_op jit(solution)/shard_map/all_to_all | solution.py:243
  78.2 2.5 %broadcast_in_dim.24 = bf16[64,2,8,2304]{3,2,1,0:T(8,128)(2,1)} broadcast(bf16[64,8,2304]{2,1,0:T(8,128)(2,1)S(1)} %bitcast.27), dimensions={0,2,3} | broadcast | bytes 7077888 | tf_op jit(solution)/shard_map/broadcast_in_dim | solution.py:241
  80.7 6.0 %all-to-all-start = ((bf16[128,8,2304]{2,1,0:T(8,128)(2,1)}), bf16[128,8,2304]{2,1,0:T(8,128)(2,1)}, u32[]{:S(2)}, u32[]{:S(2)}) async-start(bf16[128,8,2304]{2,1,0:T(8,128)(2,1)} %bitcast.31), calls=%async_computation | async-start | bytes 9437184 | tf_op jit(solution)/shard_map/all_to_all | solution.py:243
  86.7 6.8 %copy.17 = bf16[1,2880,720]{2,1,0:T(8,128)(2,1)} copy(bf16[1,2880,720]{1,2,0:T(8,128)(2,1)} %param.13) | data formatting | bytes 8294400 | tf_op args[5]
  93.5 6.6 %copy.18 = bf16[1,2880,720]{2,1,0:T(8,128)(2,1)} copy(bf16[1,2880,720]{1,2,0:T(8,128)(2,1)} %param.14) | data formatting | bytes 8294400 | tf_op args[6]
  100.1 6.6 %copy.19 = bf16[1,2880,720]{2,1,0:T(8,128)(2,1)} copy(bf16[1,2880,720]{1,2,0:T(8,128)(2,1)} %param.15) | data formatting | bytes 8294400 | tf_op args[7]
  106.7 15.2 %shard_map.120 = (bf16[768,2880]{1,0:T(8,128)(2,1)}, bf16[768,720]{1,0:T(8,128)(2,1)}, f32[768,720]{1,0:T(8,128)}, f32[768,720]{1,0:T(8,128)}) custom-call(bf16[1024,2304]{1,0:T(8,128)(2,1)} %bitcast.34, bf16[2880,720]{1,0:T(8,128)(2,1)} %bitcast.35, bf16[2880,720]{1,0:T(8,128)(2,1)} %bitcast.37), custom_call_target="tpu_custom_call" | custom-call | flops 6370099200 | bytes 20971520 | tf_op jit(solution)/shard_map/pallas_call | solution.py:116
  121.8 22.4 %all-to-all-done = bf16[128,8,2304]{2,1,0:T(8,128)(2,1)} async-done(((bf16[128,8,2304]{2,1,0:T(8,128)(2,1)}), bf16[128,8,2304]{2,1,0:T(8,128)(2,1)}, u32[]{:S(2)}, u32[]{:S(2)}) %all-to-all-start) | async-done | bytes 4718624 | tf_op jit(solution)/shard_map/all_to_all | solution.py:243
  144.3 29.9 %shard_map.121 = (bf16[768,2880]{1,0:T(8,128)(2,1)}, bf16[768,720]{1,0:T(8,128)(2,1)}, bf16[768,720]{1,0:T(8,128)(2,1)}, bf16[1024,2304]{1,0:T(8,128)(2,1)}) custom-call(bf16[1024,2304]{1,0:T(8,128)(2,1)} %bitcast.5.msg_ref, bf16[2880,720]{1,0:T(8,128)(2,1)} %bitcast.36, bf16[2880,720]{1,0:T(8,128)(2,1)} %bitcast.38, bf16[2880,720]{1,0:T(8,128)(2,1)} %bitcast.39, ...), custom_call_target="tpu_custom_call" | custom-call | flops 9555148800 | bytes 31457280 | tf_op jit(solution)/shard_map/pallas_call | solution.py:166
  174.2 6.1 %all-to-all-start.2 = ((bf16[128,8,2304]{2,1,0:T(8,128)(2,1)}), bf16[128,8,2304]{2,1,0:T(8,128)(2,1)}, u32[]{:S(2)}, u32[]{:S(2)}) async-start(bf16[128,8,2304]{2,1,0:T(8,128)(2,1)} %bitcast.33), calls=%async_computation.2 | async-start | bytes 9437184 | tf_op jit(solution)/shard_map/all_to_all | solution.py:249
  180.6 7.8 %fusion.2 = bf16[1,2880,720]{1,2,0:T(8,128)(2,1)} fusion(bf16[768,2880]{1,0:T(8,128)(2,1)} %get-tuple-element.28, bf16[768,720]{1,0:T(8,128)(2,1)S(1)} %copy-done.4), kind=kOutput, calls=%fused_computation.5 | convolution fusion | flops 3187123200 | bytes 9676800 | tf_op jit(solution)/shard_map/dot_general | solution.py:253
  188.4 7.8 %fusion.1 = bf16[1,2880,720]{1,2,0:T(8,128)(2,1)} fusion(bf16[768,2880]{1,0:T(8,128)(2,1)} %get-tuple-element.25, bf16[768,720]{1,0:T(8,128)(2,1)S(1)} %copy-done.6), kind=kOutput, calls=%fused_computation.4 | convolution fusion | flops 3187123200 | bytes 9676800 | tf_op jit(solution)/shard_map/dot_general | solution.py:255
  196.3 5.2 %fusion = bf16[1,2880,720]{1,2,0:T(8,128)(2,1)} fusion(bf16[768,2880]{1,0:T(8,128)(2,1)S(1)} %bitcast.41, bf16[768,720]{1,0:T(8,128)(2,1)S(1)} %copy-done.5), kind=kOutput, calls=%fused_computation.3 | convolution fusion | flops 3187123200 | bytes 9676800 | tf_op jit(solution)/shard_map/dot_general | solution.py:254
  201.5 36.4 %all-to-all-done.2 = bf16[128,8,2304]{2,1,0:T(8,128)(2,1)} async-done(((bf16[128,8,2304]{2,1,0:T(8,128)(2,1)}), bf16[128,8,2304]{2,1,0:T(8,128)(2,1)}, u32[]{:S(2)}, u32[]{:S(2)}) %all-to-all-start.2) | async-done | bytes 4718624 | tf_op jit(solution)/shard_map/all_to_all | solution.py:249
  237.9 4.8 %shard_map.122 = (bf16[128,2880]{1,0:T(8,128)(2,1)S(1)}, f32[128,4]{1,0:T(8,128)S(1)}) custom-call(s32[128,4]{1,0:T(8,128)S(1)} %copy.20.expert_ref, s32[128,4]{1,0:T(8,128)S(1)} %copy.21.slot_ref, f32[128,4]{1,0:T(8,128)S(1)} %get-tuple-element.35.prob_ref, bf16[1024,2304]{1,0:T(8,128)(2,1)} %bitcast.13.back_ref), custom_call_target="tpu_custom_call" | custom-call | tf_op jit(solution)/shard_map/pallas_call | solution.py:221
  242.7 1.1 copy.22
  243.8 0.7 copy.23
  (22 shorter events, 0.5 us)
Async XLA Ops:
  4.5 0.7 copy-start
  5.2 0.7 copy-start.2
  80.7 63.6 %all-to-all-start = ((bf16[128,8,2304]{2,1,0:T(8,128)(2,1)}), bf16[128,8,2304]{2,1,0:T(8,128)(2,1)}, u32[]{:S(2)}, u32[]{:S(2)}) async-start(bf16[128,8,2304]{2,1,0:T(8,128)(2,1)} %bitcast.31), calls=%async_computation | async-start | bytes 9437184 | tf_op jit(solution)/shard_map/all_to_all | solution.py:243
  174.1 6.2 %copy-start.1 = (s32[128,4]{0,1:T(4,128)S(1)}, s32[128,4]{0,1:T(4,128)}, u32[]{:S(2)}) copy-start(s32[128,4]{0,1:T(4,128)} %param.10) | copy-start | bytes 6148
  174.1 6.3 %copy-start.3 = (s32[128,4]{0,1:T(4,128)S(1)}, s32[128,4]{0,1:T(4,128)}, u32[]{:S(2)}) copy-start(s32[128,4]{0,1:T(4,128)} %param.11) | copy-start | bytes 6148
  174.2 6.4 %copy-start.4 = (bf16[768,720]{1,0:T(8,128)(2,1)S(1)}, bf16[768,720]{1,0:T(8,128)(2,1)}, u32[]{:S(2)}) copy-start(bf16[768,720]{1,0:T(8,128)(2,1)} %get-tuple-element.19.hidden_ref) | copy-start | bytes 3317764
  174.2 63.7 %all-to-all-start.2 = ((bf16[128,8,2304]{2,1,0:T(8,128)(2,1)}), bf16[128,8,2304]{2,1,0:T(8,128)(2,1)}, u32[]{:S(2)}, u32[]{:S(2)}) async-start(bf16[128,8,2304]{2,1,0:T(8,128)(2,1)} %bitcast.33), calls=%async_computation.2 | async-start | bytes 9437184 | tf_op jit(solution)/shard_map/all_to_all | solution.py:249
  180.6 7.9 %copy-start.6 = (bf16[768,720]{1,0:T(8,128)(2,1)S(1)}, bf16[768,720]{1,0:T(8,128)(2,1)}, u32[]{:S(2)}) copy-start(bf16[768,720]{1,0:T(8,128)(2,1)} %get-tuple-element.27) | copy-start | bytes 3317764
  180.6 15.7 %slice-start = ((s8[4521984]{0:T(1024)(128)(4,1)}), s8[4194304]{0:T(1024)(128)(4,1)S(1)}, s32[]{:S(2)}) async-start(s8[4521984]{0:T(1024)(128)(4,1)} %bitcast.40), calls=%async_computation.3 | async-start | bytes 8388608
  188.4 7.8 %slice-start.1 = ((s8[4521984]{0:T(1024)(128)(4,1)}), s8[327680]{0:T(1024)(128)(4,1)S(1)}, s32[]{:S(2)}) async-start(s8[4521984]{0:T(1024)(128)(4,1)} %bitcast.40), calls=%async_computation.4 | async-start | bytes 655360
  188.4 7.8 %copy-start.5 = (bf16[768,720]{1,0:T(8,128)(2,1)S(1)}, bf16[768,720]{1,0:T(8,128)(2,1)}, u32[]{:S(2)}) copy-start(bf16[768,720]{1,0:T(8,128)(2,1)} %get-tuple-element.26) | copy-start | bytes 3317764

commit v2 on v1

--- a/solution.py
+++ b/solution.py
@@ -28,55 +28,302 @@
     return lax.broadcasted_iota(jnp.int32, shape, dim)
 
 
-def pack_kernel(expert_ref, slot_ref, prob_ref, tok_ref, cot_ref, rows_ref, wt_ref, rem_ref):
-    toks = tok_ref.shape[0]
-    rest = tok_ref.shape[1] - MAIN
+def pack_kernel(code_ref, tok_ref, rows_ref, rem_ref):
+    width, toks = tok_ref.shape
     total = rows_ref.shape[0]
-    row = iota((total, toks), 0)
-    zero = jnp.zeros((total, toks), F32)
-    one, par, orem, prem = zero, zero, [zero] * 3, [zero] * 3
-    for k in range(expert_ref.shape[0]):
-        expert, slot, prob = expert_ref[k : k + 1, :], slot_ref[k : k + 1, :], prob_ref[k : k + 1, :]
-        kept = slot >= 0
-        hit = row == jnp.where(kept, expert * MROWS + slot, -1)
-        one = jnp.where(hit, 1.0, one)
-        par = jnp.where(hit, prob, par)
-        high = jnp.where(slot >= 3, 1, 0)
-        place = expert * MROWS + CAP + high
-        for j in range(3):
-            hit = row == jnp.where(kept & (slot - 3 * high == j), place, -1)
-            orem[j] = jnp.where(hit, 1.0, orem[j])
-            prem[j] = jnp.where(hit, prob, prem[j])
+    row = iota((total, 1), 0)
+    slot = row % MROWS
+    message = row // MROWS
     rem_ref[...] = jnp.zeros_like(rem_ref)
-    for src, dst, main, extra in ((tok_ref, rows_ref, one, orem), (cot_ref, wt_ref, par, prem)):
-        rem_ref[:, :rest] = src[:, MAIN:]
-        main = main.astype(BF)
-        for j in range(3):
-            cols = slice(j * CHUNK, (j + 1) * CHUNK)
-            part = dot(main, src[:, cols]) + dot(extra[j].astype(BF), rem_ref[...])
-            dst[:, cols] = part.astype(BF)
-        cols = slice(3 * CHUNK, MAIN)
-        dst[:, cols] = dot(main, src[:, cols]).astype(BF)
-
-
-def pack(expert_t, slot_t, prob_t, tokens, cotangent, experts):
-    shape = jax.ShapeDtypeStruct((experts * MROWS, MAIN), BF)
+    rem_ref[: width - MAIN, :] = tok_ref[MAIN:, :]
+    place_into(rows_ref, message, slot, [(code_ref[k : k + 1, :], None) for k in range(code_ref.shape[0])], tok_ref, rem_ref)
+
+
+def place_into(dst, expert, slot, choices, src, rest):
+    toks = src.shape[1]
+    none = jnp.zeros((expert.shape[0], toks), F32)
+
+    def matrix(wanted):
+        out = none
+        for code, prob in choices:
+            out = jnp.where(code == wanted, 1.0 if prob is None else prob, out)
+        return out.astype(BF)
+
+    main = matrix(jnp.where(slot < CAP, expert * MROWS + slot, -2).astype(code_type(choices)))
+    for j in range(3):
+        cols = slice(j * CHUNK, (j + 1) * CHUNK)
+        extra = matrix(jnp.where(slot >= CAP, expert * MROWS + 3 * (slot - CAP) + j, -2).astype(code_type(choices)))
+        dst[:, cols] = (dot_nt(main, src[cols, :]) + dot_nt(extra, rest[...])).astype(BF)
+    dst[:, 3 * CHUNK :] = dot_nt(main, src[3 * CHUNK : MAIN, :]).astype(BF)
+
+
+def code_type(choices):
+    return choices[0][0].dtype
+
+
+def pack(code, tokens_t, experts):
     return pl.pallas_call(
         pack_kernel,
-        out_shape=(shape, shape),
-        scratch_shapes=[pltpu.VMEM((tokens.shape[0], CHUNK), BF)],
+        out_shape=jax.ShapeDtypeStruct((experts * MROWS, MAIN), BF),
+        scratch_shapes=[pltpu.VMEM((CHUNK, tokens_t.shape[1]), BF)],
         compiler_params=pltpu.CompilerParams(vmem_limit_bytes=40 * 2**20),
-    )(expert_t, slot_t, prob_t, tokens, cotangent)
-
-
-def picks(out_rows, in_rows, wide):
+    )(code, tokens_t)
+
+
+STEPS = (1, 3, 2)
+LINE = ((1, 0), (3, 0), (2, 0), (1, 1), (3, 1), (2, 1), (0, 1))
+MESH = pl.DeviceIdType.MESH
+HALF = MAIN // 2
+PARTS = 2
+BLOCKS = 8 // PARTS
+
+
+def exchange_kernel(table_ref, rows_ref, cot_ref, rows_out, wt_out, *scratch):
+    (relay_a, held_a, relay_b, cots, tables, sent, rest, block_buf) = scratch[:8]
+    (tab_s, tab_r, cot_s, cot_r, a1_s, a1_r, a2_s, a2_r, a3_s, a3_r, b1_s, b1_r, b2_s, b2_r, own) = scratch[8:]
+    e, d = lax.axis_index("expert"), lax.axis_index("dp")
+    z, y, x, c = e // 16, (e // 4) % 4, d * 2 + (e // 2) % 2, e % 2
+    xc, sub = x * 2 + c, (x % 2) * 2 + c
+
+    def device(dz, dy, dx=0, dc=0):
+        ox = (x + dx) % 4
+        return ((((z + dz) % 4) * 4 + (y + dy) % 4) * 2 + ox % 2) * 2 + (c + dc) % 2, ox // 2
+
+    barrier = pltpu.get_barrier_semaphore()
+    for step in STEPS:
+        pl.semaphore_signal(barrier, inc=1, device_id=device(step, 0), device_id_type=MESH)
+        pl.semaphore_signal(barrier, inc=1, device_id=device(0, step), device_id_type=MESH)
+    for off in LINE:
+        pl.semaphore_signal(barrier, inc=1, device_id=device(0, 0, *off), device_id_type=MESH)
+    pl.semaphore_wait(barrier, 2 * len(STEPS) + len(LINE))
+
+    started = []
+
+    def send(src, dst, ssem, rsem, target):
+        copy = pltpu.make_async_remote_copy(
+            src_ref=src, dst_ref=dst, send_sem=ssem, recv_sem=rsem, device_id=target, device_id_type=MESH
+        )
+        copy.start()
+        started.append(copy)
+        return copy
+
+    local = []
+
+    def keep(src, dst, sem):
+        copy = pltpu.make_async_copy(src, dst, sem)
+        copy.start()
+        local.append(copy)
+        return copy
+
+    mine = (z, y)
+    halves = (pl.ds(0, HALF), pl.ds(HALF, HALF))
+
+    def at(h, first, second):
+        return (first, second) if h == 0 else (second, first)
+
+    def first_step(h, step):
+        return device(step, 0) if h == 0 else device(0, step)
+
+    def second_step(h, step):
+        return device(0, step) if h == 0 else device(step, 0)
+
+    def pick(ref, h, first, second, *more):
+        one, two = at(h, first, second)
+        return ref.at[(one, two, *more)]
+
+    every = slice(None)
+    keep(cot_ref, cots.at[xc], own.at[0])
+    keep(table_ref, tables.at[xc], own.at[1])
+    a1 = [[None] * 3, [None] * 3]
+    a2 = [[[None] * 3 for _ in range(4)] for _ in range(2)]
+    for h in range(2):
+        keep(rows_ref.at[z, y, :, :, halves[h]], relay_a.at[h, mine[h], mine[1 - h]], own.at[2 + h])
+    for i, off in enumerate(LINE):
+        tab = send(table_ref, tables.at[xc], tab_s.at[i], tab_r.at[i], device(0, 0, *off))
+    tab_copies = started[-len(LINE) :]
+    tail = cot_ref.shape[0] // 2
+    parts = (pl.ds(0, tail), pl.ds(tail, tail))
+
+    def send_cot(src, dst, k, target):
+        return send(src, dst, cot_s.at[k], cot_r.at[k], target)
+
+    near = [send_cot(cot_ref, cots.at[xc], i, device(0, 0, step)) for i, step in enumerate((1, 3))]
+    for i, step in enumerate(STEPS):
+        for h in range(2):
+            to = (mine[h] + step) % 4
+            a1[h][i] = send(
+                pick(rows_ref, h, to, every, every, every, halves[h]),
+                relay_a.at[h, mine[h]],
+                a1_s.at[h, i],
+                a1_r.at[h, i],
+                first_step(h, step),
+            )
+    other_core = [send_cot(cot_ref, cots.at[xc], 4, device(0, 0, 0, 1))]
+
+    def forward_rows(h, i, source):
+        for j, step in enumerate(STEPS):
+            to = (mine[1 - h] + step) % 4
+            if source is None:
+                src = pick(rows_ref, h, mine[h], to, every, every, halves[h])
+                place = mine[h]
+            else:
+                src = relay_a.at[h, source, to]
+                place = source
+            a2[h][i][j] = send(src, held_a.at[h, mine[1 - h], place], a2_s.at[h, i, j], a2_r.at[h, i, j], second_step(h, step))
+
+    for h in range(2):
+        forward_rows(h, 3, None)
+    def forward_a1(i):
+        for h in range(2):
+            a1[h][i].wait_recv()
+            forward_rows(h, i, (mine[h] - STEPS[i]) % 4)
+
+    forward_a1(0)
+    forward_a1(1)
+    far = []
+    for i, step in enumerate((1, 3)):
+        block = ((x - step) % 4) * 2 + c
+        near[i].wait_recv()
+        far.append(send_cot(cots.at[block, parts[i]], cots.at[block, parts[i]], 2 + i, device(0, 0, step)))
+        other_core.append(send_cot(cots.at[block], cots.at[block], 5 + i, device(0, 0, 0, 1)))
+    forward_a1(2)
+    block = ((x + 2) % 4) * 2 + c
+    for i in range(2):
+        far[i].wait_recv()
+        other_core.append(send_cot(cots.at[block, parts[i]], cots.at[block, parts[i]], 7 + i, device(0, 0, 0, 1)))
+
+    def spread_rows(h, group, source, place):
+        where = pick(rows_out, h, every, place, xc, every, halves[h])
+        for k, off in enumerate(LINE):
+            ox, oc = (x + off[0]) % 4, (c + off[1]) % 2
+            send(
+                source.at[:, (ox % 2) * 2 + oc],
+                where,
+                a3_s.at[h, group, k],
+                a3_r.at[h, group, k],
+                device(0, 0, *off),
+            )
+        keep(source.at[:, sub], where, own.at[4 + 4 * h + group])
+
+    for copy in local[:4]:
+        copy.wait()
+    for h in range(2):
+        spread_rows(h, 3, relay_a.at[h, :, mine[1 - h]], mine[1 - h])
+
+    rest[...] = jnp.zeros_like(rest)
+    width = cot_ref.shape[0]
+    row = iota((16 * MROWS, 1), 0)
+
+    def make_block(b):
+        rest[: width - MAIN, :] = cots[b, MAIN:, :]
+        choices = [(tables[b, k : k + 1, :], tables[b, 4 + k : 5 + k, :]) for k in range(4)]
+        place_into(block_buf, (row // MROWS) * 4 + sub, row % MROWS, choices, cots.at[b], rest)
+        sent[:, :, b] = block_buf[...].reshape(4, 4, MROWS, MAIN)
+
+    for copy in tab_copies + other_core:
+        copy.wait_recv()
+    b1 = [[[None] * 3, [None] * 3] for _ in range(PARTS)]
+    b2 = [[[[None] * 3 for _ in range(4)] for _ in range(2)] for _ in range(PARTS)]
+
+    def forward_wts(p, h, i, source):
+        blocks = pl.ds(p * BLOCKS, BLOCKS)
+        for j, step in enumerate(STEPS + (0,)):
+            to = (mine[1 - h] + step) % 4
+            if source is None:
+                src = pick(sent, h, mine[h], to, blocks, every, halves[h])
+                place = mine[h]
+            else:
+                src = relay_b.at[h, source, to, blocks]
+                place = source
+            dst = pick(wt_out, h, place, mine[1 - h], blocks, every, halves[h])
+            if step:
+                b2[p][h][i][j] = send(src, dst, b2_s.at[p, h, i, j], b2_r.at[p, h, i, j], second_step(h, step))
+            else:
+                keep(src, dst, own.at[12 + (p * 2 + h) * 4 + i])
+
+    for p in range(PARTS):
+        blocks = pl.ds(p * BLOCKS, BLOCKS)
+
+        @pl.loop(p * BLOCKS, (p + 1) * BLOCKS)
+        def _(b):
+            make_block(b)
+
+        for i, step in enumerate(STEPS):
+            for h in range(2):
+                to = (mine[h] + step) % 4
+                b1[p][h][i] = send(
+                    pick(sent, h, to, every, blocks, every, halves[h]),
+                    relay_b.at[h, mine[h], :, blocks],
+                    b1_s.at[p, h, i],
+                    b1_r.at[p, h, i],
+                    first_step(h, step),
+                )
+        for h in range(2):
+            forward_wts(p, h, 3, None)
+
+    for j, step in enumerate(STEPS):
+        for h in range(2):
+            for i in range(4):
+                a2[h][i][j].wait_recv()
+            place = (mine[1 - h] - step) % 4
+            spread_rows(h, j, held_a.at[h, place], place)
+
+    for p in range(PARTS):
+        for i, step in enumerate(STEPS):
+            for h in range(2):
+                b1[p][h][i].wait_recv()
+                forward_wts(p, h, i, (mine[h] - step) % 4)
+
+    early = {id(copy) for copy in tab_copies + near + far + other_core}
+    for group in a1 + [v for half in a2 for v in half] + [v for part in b1 for v in part]:
+        early |= {id(copy) for copy in group}
+    for copy in local[4:]:
+        copy.wait()
+    for copy in started:
+        if id(copy) not in early:
+            copy.wait_recv()
+    for copy in started:
+        copy.wait_send()
+
+
+def exchange(table, rows_msg, cot_t):
+    out = jax.ShapeDtypeStruct((4, 4, 8, MROWS, MAIN), BF)
+    anywhere = pl.BlockSpec(memory_space=pl.ANY)
+    shapes = [(7,), (9,), (2, 3), (2, 4, 3), (2, 4, 7), (PARTS, 2, 3), (PARTS, 2, 4, 3)]
+    sems = [pltpu.SemaphoreType.DMA(shape) for shape in shapes for _ in range(2)]
+    return pl.pallas_call(
+        exchange_kernel,
+        in_specs=[anywhere] * 3,
+        out_specs=[anywhere] * 2,
+        out_shape=[out, out],
+        scratch_shapes=[
+            pltpu.VMEM((2, 4, 4, 4, MROWS, HALF), BF),
+            pltpu.VMEM((2, 4, 4, 4, MROWS, HALF), BF),
+            pltpu.VMEM((2, 4, 4, 8, MROWS, HALF), BF),
+            pltpu.VMEM((8, *cot_t.shape), BF),
+            pltpu.VMEM((8, *table.shape), F32),
+            pltpu.VMEM((4, 4, 8, MROWS, MAIN), BF),
+            pltpu.VMEM((CHUNK, cot_t.shape[1]), BF),
+            pltpu.VMEM((16 * MROWS, MAIN), BF),
+            *sems,
+            pltpu.SemaphoreType.DMA((12 + 8 * PARTS,)),
+        ],
+        compiler_params=pltpu.CompilerParams(collective_id=0, has_side_effects=True, vmem_limit_bytes=48 * 2**20),
+    )(table, rows_msg.reshape(4, 4, 4, MROWS, MAIN), cot_t)
+
+
+def picks(out_rows, in_rows, wide, reorder=False):
     if wide:
         q, o = iota((out_rows, in_rows), 0), iota((out_rows, in_rows), 1)
     else:
         o, q = iota((out_rows, in_rows), 0), iota((out_rows, in_rows), 1)
     message = o // CAP
     slot = o - CAP * message
-    base = q - MROWS * message
+    if reorder:
+        at = message % 8
+        base = q - MROWS * (message - at + (at % 4) * 2 + at // 4)
+    else:
+        base = q - MROWS * message
     high = jnp.where(slot >= 3, 1, 0)
     main = jnp.where(base == slot, 1.0, 0.0).astype(BF)
     last = base == CAP + high
@@ -96,8 +343,8 @@
 
 def forward_kernel(msg_ref, gate_ref, up_ref, rows_ref, hidden_ref, glu_ref, slope_ref):
     unpack_into(msg_ref, rows_ref)
-    gate = dot(rows_ref[...], gate_ref[...])
-    up = dot(rows_ref[...], up_ref[...]) + 1.0
+    gate = dot_nt(rows_ref[...], gate_ref[...])
+    up = dot_nt(rows_ref[...], up_ref[...]) + 1.0
     sig = jax.nn.sigmoid(ALPHA * gate)
     glu = gate * sig
     hidden_ref[...] = (up * glu).astype(BF)
@@ -106,12 +353,12 @@
 
 
 def forward(msgs, gate_w, up_w, tile):
-    width, units = gate_w.shape
+    units, width = gate_w.shape
     groups = msgs.shape[0] // MROWS
     steps = groups * CAP // tile
     wide = tile // CAP * MROWS
     block = lambda cols: pl.BlockSpec((tile, cols), lambda i: (i, 0))
-    whole = pl.BlockSpec((width, units), lambda i: (0, 0))
+    whole = pl.BlockSpec((units, width), lambda i: (0, 0))
     rows = groups * CAP
     return pl.pallas_call(
         forward_kernel,
@@ -135,13 +382,13 @@
     tile = wt_ref.shape[0]
     width = wt_ref.shape[1]
     unpack_into(msg_ref, wt_ref)
-    hgrad = dot(wt_ref[...], down_ref[...])
+    hgrad = dot_nt(wt_ref[...], down_ref[...])
     share = jnp.sum(hgrad * hidden_ref[...].astype(F32), axis=1, keepdims=True)
     ug_ref[...] = (hgrad * glu_ref[...]).astype(BF)
     gg_ref[...] = (hgrad * slope_ref[...]).astype(BF)
     full_ref[:, width:] = jnp.zeros((tile, full_ref.shape[1] - width), BF)
-    full_ref[:, :width] = (dot_nt(gg_ref[...], gate_ref[...]) + dot_nt(ug_ref[...], up_ref[...])).astype(BF)
-    main, rem, last = picks(out_ref.shape[0], tile, True)
+    full_ref[:, :width] = (dot(gg_ref[...], gate_ref[...]) + dot(ug_ref[...], up_ref[...])).astype(BF)
+    main, rem, last = picks(out_ref.shape[0], tile, True, True)
     tail = full_ref[:, MAIN : MAIN + CHUNK]
     for j in range(3):
         cols = slice(j * CHUNK, (j + 1) * CHUNK)
@@ -157,11 +404,11 @@
 
 
 def backward(msgs, gate_w, up_w, down_w, hidden, glu, slope, tile):
-    width, units = gate_w.shape
+    units, width = gate_w.shape
     rows = hidden.shape[0]
     wide = tile // CAP * MROWS
     block = lambda cols: pl.BlockSpec((tile, cols), lambda i: (i, 0))
-    whole = pl.BlockSpec((width, units), lambda i: (0, 0))
+    whole = pl.BlockSpec((units, width), lambda i: (0, 0))
     packed = pl.BlockSpec((wide, MAIN), lambda i: (i, 0))
     return pl.pallas_call(
         backward_kernel,
@@ -233,17 +480,14 @@
     copies = lax.axis_size("dp")
     devices = experts * copies
     width = tokens.shape[1]
-    gate_w, up_w, down_w = w_gate[0], w_up[0], w_down[0]
+    gate_w, up_w, down_w = w_gate[0].T, w_up[0].T, w_down[0].T
     rounded = probs.astype(BF).astype(F32)
-    rows_msg, wt_msg = pack(expert_ids.T, slots.T, rounded.T, tokens, cotangent, experts)
-
-    def spread(msg):
-        msg = jnp.broadcast_to(msg.reshape(experts, 1, MROWS, MAIN), (experts, copies, MROWS, MAIN))
-        msg = msg.reshape(devices, MROWS, MAIN)
-        return lax.all_to_all(msg, ("expert", "dp"), split_axis=0, concat_axis=0, tiled=True)
-
-    rows_in = spread(rows_msg).reshape(devices * MROWS, MAIN)
-    wt_in = spread(wt_msg).reshape(devices * MROWS, MAIN)
+    code = jnp.where(slots >= 0, expert_ids * MROWS + slots, -1).T
+    rows_msg = pack(code, tokens.T, experts)
+    table = jnp.concatenate([code.astype(F32), rounded.T], axis=0)
+    rows_in, wt_in = exchange(table, rows_msg, cotangent.T)
+    rows_in = rows_in.reshape(devices * MROWS, MAIN)
+    wt_in = wt_in.reshape(devices * MROWS, MAIN)
     rows, hidden, glu, slope = forward(rows_in, gate_w, up_w, 192)
     weighted, gate_grad, up_grad, packed = backward(wt_in, gate_w, up_w, down_w, hidden, glu, slope, 192)
     back = lax.all_to_all(

time: 245 us -> 220 us (0.90)
  Pallas kernels: 52.5 us -> 147 us
  blocking collectives: 69.4 us -> 0 us
  local copies, waits for them, and re-layouts: 29.3 us -> 4.47 us
  waiting for transfers between devices: 58.8 us -> 36.6 us
  starting transfers between devices: 12.1 us -> 8.37 us
    pallas_call x1 -> x2, Pallas kernels: 2.66 us -> 94 us  [the longest x1 92.6 us: exchange(): pl.pallas_call(exchange_kernel, in_specs=[anywhere] * 3, out_specs=[anywh...]
    all_to_all x1 -> x0, blocking collectives: 69.4 us -> none  [spread(): lax.all_to_all(msg, ('expert', 'dp'), split_axis=0, concat_axis=0, tiled=...]
    all_to_all x1 -> x0, waiting for transfers between devices: 22.4 us -> none  [spread(): lax.all_to_all(msg, ('expert', 'dp'), split_axis=0, concat_axis=0, tiled=...]
    unnamed x27 -> x22, local copies, waits for them, and re-layouts: 26.3 us -> 4.27 us
    all_to_all x1 -> x0, starting transfers between devices: 5.96 us -> none  [spread(): lax.all_to_all(msg, ('expert', 'dp'), split_axis=0, concat_axis=0, tiled=...]
    broadcast_in_dim x2 -> x0, local copies, waits for them, and re-layouts: 2.8 us -> none  [spread(): jnp.broadcast_to(msg.reshape(experts, 1, MROWS, MAIN), (experts, copies,...]
    pallas_call x1, Pallas kernels: 15.2 us -> 17.7 us  [forward(): pl.pallas_call(forward_kernel, grid=(steps,), in_specs=[pl.BlockSpec((wid...]
  transfers between devices with their start and end apart: 2 -> 1, of which waited for: 2 -> 1; matrix products, arithmetic and copies ran while one was open for 17% -> 10% of each run, Pallas kernels for 6% -> 0%
where the time goes in v2:
time: 220 us; the launch traced here: 219 us
  Pallas kernels  147 us (67%)
  waiting for transfers between devices  36.6 us (17%)
  matrix products  20.9 us (10%)
  starting transfers between devices  8.37 us (4%)
  local copies, waits for them, and re-layouts  4.47 us (2%)
    pallas_call x1, Pallas kernels, exchange(): pl.pallas_call(exchange_kernel, in_specs=[anywhere] * 3, out_specs=[anywh...  92.6 us
    all_to_all x1, waiting for transfers between devices, body(): lax.all_to_all(packed.reshape(devices, MROWS, MAIN), ('expert', 'dp'), sp...  36.6 us
    pallas_call x1, Pallas kernels, backward(): pl.pallas_call(backward_kernel, grid=(rows // tile,), in_specs=[packed, w...  30.2 us
    pallas_call x1, Pallas kernels, forward(): pl.pallas_call(forward_kernel, grid=(steps,), in_specs=[pl.BlockSpec((wid...  17.7 us
    all_to_all x1, starting transfers between devices, body(): lax.all_to_all(packed.reshape(devices, MROWS, MAIN), ('expert', 'dp'), sp...  8.37 us
    dot_general x1, matrix products, body(): lax.dot_general(weighted, hidden, contract_rows, preferred_element_type=F32)  7.85 us
    dot_general x1, matrix products, body(): lax.dot_general(rows, up_grad, contract_rows, preferred_element_type=F32)  7.79 us
    dot_general x1, matrix products, body(): lax.dot_general(rows, gate_grad, contract_rows, preferred_element_type=F32)  5.23 us
  transfers between devices with their start and end apart: 1, of which 1 were waited for; matrix products, arithmetic and copies ran while one was open for 10% of the time, Pallas kernels for 0%

profile of v2, /device:TPU:0, one launch (start us, length us, event | category | flops | bytes accessed | tf_op | source)
XLA Modules:
  0.0 219.3 jit_solution(9930468509743948238)
XLA Ops:
  0.6 0.7 convert_element_type.18
  1.3 0.1 copy.25
  1.5 0.1 copy.26
  1.5 0.7 fusion.3
  2.3 0.0 copy-start
  2.3 1.1 copy-done
  3.4 1.4 shard_map.119
  4.8 0.0 copy-start.1
  4.8 1.1 copy-done.1
  5.9 92.6 %shard_map.120 = (bf16[4,4,8,8,2304]{4,3,2,1,0:T(8,128)(2,1)}, bf16[4,4,8,8,2304]{4,3,2,1,0:T(8,128)(2,1)}) custom-call(f32[8,128]{1,0:T(8,128)S(1)} %pad_maximum_fusion.table_ref, bf16[4,4,4,8,2304]{4,3,2,1,0:T(8,128)(2,1)S(1)} %bitcast.33, bf16[2880,128]{1,0:T(8,128)(2,1)S(1)} %bitcast.35), custom_call_target="tpu_custom_call" | custom-call | tf_op jit(solution)/shard_map/pallas_call | solution.py:294
  98.6 17.7 %shard_map.121 = (bf16[768,2880]{1,0:T(8,128)(2,1)}, bf16[768,720]{1,0:T(8,128)(2,1)}, f32[768,720]{1,0:T(8,128)}, f32[768,720]{1,0:T(8,128)}) custom-call(bf16[1024,2304]{1,0:T(8,128)(2,1)} %bitcast.38, bf16[720,2880]{1,0:T(8,128)(2,1)} %bitcast.39, bf16[720,2880]{1,0:T(8,128)(2,1)} %bitcast.41), custom_call_target="tpu_custom_call" | custom-call | flops 6370099200 | bytes 20971520 | tf_op jit(solution)/shard_map/pallas_call | solution.py:363
  116.3 30.2 %shard_map.122 = (bf16[768,2880]{1,0:T(8,128)(2,1)}, bf16[768,720]{1,0:T(8,128)(2,1)}, bf16[768,720]{1,0:T(8,128)(2,1)}, bf16[1024,2304]{1,0:T(8,128)(2,1)}) custom-call(bf16[1024,2304]{1,0:T(8,128)(2,1)} %bitcast.37, bf16[720,2880]{1,0:T(8,128)(2,1)} %bitcast.40, bf16[720,2880]{1,0:T(8,128)(2,1)} %bitcast.42, bf16[720,2880]{1,0:T(8,128)(2,1)} %bitcast.43, ...), custom_call_target="tpu_custom_call" | custom-call | flops 9555148800 | bytes 31457280 | tf_op jit(solution)/shard_map/pallas_call | solution.py:413
  146.5 0.0 copy-start.3
  146.5 0.0 copy-start.4
  146.5 8.4 %all-to-all-start = ((bf16[128,8,2304]{2,1,0:T(8,128)(2,1)}), bf16[128,8,2304]{2,1,0:T(8,128)(2,1)}, u32[]{:S(2)}, u32[]{:S(2)}) async-start(bf16[128,8,2304]{2,1,0:T(8,128)(2,1)} %bitcast.36), calls=%async_computation | async-start | bytes 9437184 | tf_op jit(solution)/shard_map/all_to_all | solution.py:493
  154.9 0.1 copy.27.expert_ref
  155.0 0.1 copy.28.slot_ref
  155.1 7.8 %fusion.2 = bf16[1,2880,720]{1,2,0:T(8,128)(2,1)} fusion(bf16[768,2880]{1,0:T(8,128)(2,1)} %get-tuple-element.28, bf16[768,720]{1,0:T(8,128)(2,1)S(1)} %copy-done.4), kind=kOutput, calls=%fused_computation.5 | convolution fusion | flops 3187123200 | bytes 9676800 | tf_op jit(solution)/shard_map/dot_general | solution.py:497
  163.0 7.8 %fusion.1 = bf16[1,2880,720]{1,2,0:T(8,128)(2,1)} fusion(bf16[768,2880]{1,0:T(8,128)(2,1)} %get-tuple-element.25, bf16[768,720]{1,0:T(8,128)(2,1)S(1)} %copy-done.6), kind=kOutput, calls=%fused_computation.4 | convolution fusion | flops 3187123200 | bytes 9676800 | tf_op jit(solution)/shard_map/dot_general | solution.py:499
  170.8 5.2 %fusion = bf16[1,2880,720]{1,2,0:T(8,128)(2,1)} fusion(bf16[768,2880]{1,0:T(8,128)(2,1)S(1)} %bitcast.45, bf16[768,720]{1,0:T(8,128)(2,1)S(1)} %copy-done.5), kind=kOutput, calls=%fused_computation.3 | convolution fusion | flops 3187123200 | bytes 9676800 | tf_op jit(solution)/shard_map/dot_general | solution.py:498
  176.0 36.6 %all-to-all-done = bf16[128,8,2304]{2,1,0:T(8,128)(2,1)} async-done(((bf16[128,8,2304]{2,1,0:T(8,128)(2,1)}), bf16[128,8,2304]{2,1,0:T(8,128)(2,1)}, u32[]{:S(2)}, u32[]{:S(2)}) %all-to-all-start) | async-done | bytes 4718624 | tf_op jit(solution)/shard_map/all_to_all | solution.py:493
  212.6 4.8 %shard_map.123 = (bf16[128,2880]{1,0:T(8,128)(2,1)S(1)}, f32[128,4]{1,0:T(8,128)S(1)}) custom-call(s32[128,4]{1,0:T(8,128)S(1)} %copy.27.expert_ref, s32[128,4]{1,0:T(8,128)S(1)} %copy.28.slot_ref, f32[128,4]{1,0:T(8,128)S(1)} %get-tuple-element.42.prob_ref, bf16[1024,2304]{1,0:T(8,128)(2,1)} %bitcast.16.back_ref), custom_call_target="tpu_custom_call" | custom-call | tf_op jit(solution)/shard_map/pallas_call | solution.py:468
  217.5 1.1 copy.29
  218.6 0.7 copy.30
  (15 shorter events, 0.0 us)
Async XLA Ops:
  2.3 1.1 copy-start
  4.8 1.1 copy-start.1
  146.5 8.4 %copy-start.2 = (s32[128,4]{0,1:T(4,128)S(1)}, s32[128,4]{0,1:T(4,128)}, u32[]{:S(2)}) copy-start(s32[128,4]{0,1:T(4,128)} %param.10) | copy-start | bytes 6148
  146.5 8.5 %copy-start.3 = (s32[128,4]{0,1:T(4,128)S(1)}, s32[128,4]{0,1:T(4,128)}, u32[]{:S(2)}) copy-start(s32[128,4]{0,1:T(4,128)} %param.11) | copy-start | bytes 6148
  146.5 8.6 %copy-start.4 = (bf16[768,720]{1,0:T(8,128)(2,1)S(1)}, bf16[768,720]{1,0:T(8,128)(2,1)}, u32[]{:S(2)}) copy-start(bf16[768,720]{1,0:T(8,128)(2,1)} %get-tuple-element.19.hidden_ref) | copy-start | bytes 3317764
  146.5 66.2 %all-to-all-start = ((bf16[128,8,2304]{2,1,0:T(8,128)(2,1)}), bf16[128,8,2304]{2,1,0:T(8,128)(2,1)}, u32[]{:S(2)}, u32[]{:S(2)}) async-start(bf16[128,8,2304]{2,1,0:T(8,128)(2,1)} %bitcast.36), calls=%async_computation | async-start | bytes 9437184 | tf_op jit(solution)/shard_map/all_to_all | solution.py:493
  155.1 7.9 %copy-start.6 = (bf16[768,720]{1,0:T(8,128)(2,1)S(1)}, bf16[768,720]{1,0:T(8,128)(2,1)}, u32[]{:S(2)}) copy-start(bf16[768,720]{1,0:T(8,128)(2,1)} %get-tuple-element.27) | copy-start | bytes 3317764
  155.1 15.7 %slice-start = ((s8[4521984]{0:T(1024)(128)(4,1)}), s8[4194304]{0:T(1024)(128)(4,1)S(1)}, s32[]{:S(2)}) async-start(s8[4521984]{0:T(1024)(128)(4,1)} %bitcast.44), calls=%async_computation.1 | async-start | bytes 8388608
  163.0 7.8 %slice-start.1 = ((s8[4521984]{0:T(1024)(128)(4,1)}), s8[327680]{0:T(1024)(128)(4,1)S(1)}, s32[]{:S(2)}) async-start(s8[4521984]{0:T(1024)(128)(4,1)} %bitcast.44), calls=%async_computation.2 | async-start | bytes 655360
  163.0 7.8 %copy-start.5 = (bf16[768,720]{1,0:T(8,128)(2,1)S(1)}, bf16[768,720]{1,0:T(8,128)(2,1)}, u32[]{:S(2)}) copy-start(bf16[768,720]{1,0:T(8,128)(2,1)} %get-tuple-element.26) | copy-start | bytes 3317764

commit v3 on v2

--- a/solution.py
+++ b/solution.py
@@ -331,100 +331,125 @@
     return main, rem, jnp.where(last, 1.0, 0.0).astype(BF)
 
 
-def unpack_into(src, dst):
-    main, rem, _ = picks(dst.shape[0], src.shape[0], False)
-    rest = dst.shape[1] - MAIN
-    dst[:, :MAIN] = dot(main, src[:, :MAIN]).astype(BF)
-    part = dot(rem[0], src[:, :rest])
-    for j in (1, 2):
-        part = part + dot(rem[j], src[:, j * CHUNK : j * CHUNK + rest])
-    dst[:, MAIN:] = part.astype(BF)
-
-
-def forward_kernel(msg_ref, gate_ref, up_ref, rows_ref, hidden_ref, glu_ref, slope_ref):
-    unpack_into(msg_ref, rows_ref)
-    gate = dot_nt(rows_ref[...], gate_ref[...])
-    up = dot_nt(rows_ref[...], up_ref[...]) + 1.0
-    sig = jax.nn.sigmoid(ALPHA * gate)
-    glu = gate * sig
-    hidden_ref[...] = (up * glu).astype(BF)
-    glu_ref[...] = glu
-    slope_ref[...] = up * (sig + ALPHA * glu * (1.0 - sig))
-
-
-def forward(msgs, gate_w, up_w, tile):
+TILE = 192
+WIDE = TILE // CAP * MROWS
+
+
+def expert_kernel(rows_msg, wt_msg, gate_hbm, up_hbm, down_hbm, *refs):
+    outs, bufs, sems = refs[:6], refs[6:-2], refs[-2:]
+    msg_rows, msg_wt, gate_w, up_w, down_w, rows, weighted, hidden, gate_grad, up_grad, glu, slope, full = bufs
+    rows_out, weighted_out, hidden_out, gate_grad_out, up_grad_out, packed_out = outs
+    arrive, leave = sems
+    total, width = rows.shape
+    tiles = total // TILE
+    rest = width - MAIN
+
+    def tile_of(i, size):
+        return pl.ds(pl.multiple_of(i * size, size), size)
+
+    def fetch(i, src, dst):
+        copy = pltpu.make_async_copy(src, dst, arrive.at[i])
+        copy.start()
+        return copy
+
+    def put(i, src, dst):
+        copy = pltpu.make_async_copy(src, dst, leave.at[i])
+        copy.start()
+        return copy
+
+    got_rows = fetch(0, rows_msg, msg_rows)
+    got_gate = fetch(1, gate_hbm, gate_w)
+    got_up = fetch(2, up_hbm, up_w)
+    got_wt = fetch(3, wt_msg, msg_wt)
+    got_down = fetch(4, down_hbm, down_w)
+    main, rem, _ = picks(TILE, WIDE, False)
+
+    def unpack(src, dst):
+        @pl.loop(0, tiles)
+        def _(i):
+            wide, tile = tile_of(i, WIDE), tile_of(i, TILE)
+            dst[tile, :MAIN] = dot(main, src[wide, :MAIN]).astype(BF)
+            part = dot(rem[0], src[wide, :rest])
+            for j in (1, 2):
+                part = part + dot(rem[j], src[wide, j * CHUNK : j * CHUNK + rest])
+            dst[tile, MAIN:] = part.astype(BF)
+
+    got_rows.wait()
+    unpack(msg_rows, rows)
+    puts = [put(0, rows, rows_out)]
+    got_gate.wait()
+    glu[...] = dot_nt(rows[...], gate_w[...])
+    got_up.wait()
+    slope[...] = dot_nt(rows[...], up_w[...])
+
+    @pl.loop(0, tiles)
+    def _(i):
+        tile = tile_of(i, TILE)
+        gate, up = glu[tile, :], slope[tile, :] + 1.0
+        sig = jax.nn.sigmoid(ALPHA * gate)
+        prod = gate * sig
+        hidden[tile, :] = (up * prod).astype(BF)
+        glu[tile, :] = prod
+        slope[tile, :] = up * (sig + ALPHA * prod * (1.0 - sig))
+
+    puts.append(put(1, hidden, hidden_out))
+    got_wt.wait()
+    unpack(msg_wt, weighted)
+    puts.append(put(2, weighted, weighted_out))
+    got_down.wait()
+    main_t, rem_t, last_t = picks(WIDE, TILE, True, True)
+    spare = MAIN - 3 * CHUNK
+    lane = iota((TILE, spare), 1)
+    spot = 2 * ((iota((TILE, spare), 0) % CAP) % 3)
+    hgrad = dot_nt(weighted[...], down_w[...])
+    share = jnp.sum(hgrad * hidden[...].astype(F32), axis=1, keepdims=True)
+    up_grad[...] = (hgrad * glu[...]).astype(BF)
+    gate_grad[...] = (hgrad * slope[...]).astype(BF)
+    puts.append(put(3, gate_grad, gate_grad_out))
+    puts.append(put(4, up_grad, up_grad_out))
+    full[:, width:] = jnp.zeros((total, full.shape[1] - width), BF)
+    for start in range(0, width, 768):
+        cols = slice(start, min(width, start + 768))
+        full[:, cols] = (dot(gate_grad[...], gate_w[:, cols]) + dot(up_grad[...], up_w[:, cols])).astype(BF)
+    for i in range(tiles):
+        tile, wide = slice(i * TILE, (i + 1) * TILE), slice(i * WIDE, (i + 1) * WIDE)
+        tail = full[tile, MAIN : MAIN + CHUNK]
+        for j in range(3):
+            cols = slice(j * CHUNK, (j + 1) * CHUNK)
+            msg_wt[wide, cols] = (dot(main_t, full[tile, cols]) + dot(rem_t[j], tail)).astype(BF)
+        part = share[tile, :]
+        head = part.astype(BF).astype(F32)
+        pair = jnp.where(lane == spot, head, jnp.where(lane == spot + 1, part - head, 0.0)).astype(BF)
+        cols = slice(3 * CHUNK, MAIN)
+        msg_wt[wide, cols] = (dot(main_t, full[tile, cols]) + dot(last_t, pair)).astype(BF)
+        puts.append(put(5 + i, msg_wt.at[wide], packed_out.at[wide]))
+    for copy in puts:
+        copy.wait()
+
+
+def expert(rows_msg, wt_msg, gate_w, up_w, down_w):
     units, width = gate_w.shape
-    groups = msgs.shape[0] // MROWS
-    steps = groups * CAP // tile
-    wide = tile // CAP * MROWS
-    block = lambda cols: pl.BlockSpec((tile, cols), lambda i: (i, 0))
-    whole = pl.BlockSpec((units, width), lambda i: (0, 0))
-    rows = groups * CAP
+    rows = rows_msg.shape[0] // MROWS * CAP
+    anywhere = pl.BlockSpec(memory_space=pl.ANY)
+    wide, thin = (rows, width), (rows, units)
     return pl.pallas_call(
-        forward_kernel,
-        grid=(steps,),
-        in_specs=[pl.BlockSpec((wide, MAIN), lambda i: (i, 0)), whole, whole],
-        out_specs=[block(width), block(units), block(units), block(units)],
-        out_shape=[
-            jax.ShapeDtypeStruct((rows, width), BF),
-            jax.ShapeDtypeStruct((rows, units), BF),
-            jax.ShapeDtypeStruct((rows, units), F32),
-            jax.ShapeDtypeStruct((rows, units), F32),
+        expert_kernel,
+        in_specs=[anywhere] * 5,
+        out_specs=[anywhere] * 6,
+        out_shape=[jax.ShapeDtypeStruct(shape, BF) for shape in (wide, wide, thin, thin, thin, rows_msg.shape)],
+        scratch_shapes=[
+            *[pltpu.VMEM(rows_msg.shape, BF)] * 2,
+            *[pltpu.VMEM((units, width), BF)] * 3,
+            *[pltpu.VMEM(wide, BF)] * 2,
+            *[pltpu.VMEM(thin, BF)] * 3,
+            *[pltpu.VMEM(thin, F32)] * 2,
+            pltpu.VMEM((rows, MAIN + CHUNK), BF),
+            pltpu.SemaphoreType.DMA((5,)),
+            pltpu.SemaphoreType.DMA((5 + rows // TILE,)),
         ],
-        compiler_params=pltpu.CompilerParams(vmem_limit_bytes=60 * 2**20),
-        cost_estimate=pl.CostEstimate(flops=4 * rows * width * units, bytes_accessed=20 * 2**20, transcendentals=0),
-    )(msgs, gate_w, up_w)
-
-
-def backward_kernel(
-    msg_ref, gate_ref, up_ref, down_ref, hidden_ref, glu_ref, slope_ref, wt_ref, gg_ref, ug_ref, out_ref, full_ref
-):
-    tile = wt_ref.shape[0]
-    width = wt_ref.shape[1]
-    unpack_into(msg_ref, wt_ref)
-    hgrad = dot_nt(wt_ref[...], down_ref[...])
-    share = jnp.sum(hgrad * hidden_ref[...].astype(F32), axis=1, keepdims=True)
-    ug_ref[...] = (hgrad * glu_ref[...]).astype(BF)
-    gg_ref[...] = (hgrad * slope_ref[...]).astype(BF)
-    full_ref[:, width:] = jnp.zeros((tile, full_ref.shape[1] - width), BF)
-    full_ref[:, :width] = (dot(gg_ref[...], gate_ref[...]) + dot(ug_ref[...], up_ref[...])).astype(BF)
-    main, rem, last = picks(out_ref.shape[0], tile, True, True)
-    tail = full_ref[:, MAIN : MAIN + CHUNK]
-    for j in range(3):
-        cols = slice(j * CHUNK, (j + 1) * CHUNK)
-        out_ref[:, cols] = (dot(main, full_ref[:, cols]) + dot(rem[j], tail)).astype(BF)
-    spare = MAIN - 3 * CHUNK
-    lane = iota((tile, spare), 1)
-    row = iota((tile, spare), 0)
-    head = share.astype(BF).astype(F32)
-    spot = 2 * ((row % CAP) % 3)
-    pair = jnp.where(lane == spot, head, jnp.where(lane == spot + 1, share - head, 0.0)).astype(BF)
-    cols = slice(3 * CHUNK, MAIN)
-    out_ref[:, cols] = (dot(main, full_ref[:, cols]) + dot(last, pair)).astype(BF)
-
-
-def backward(msgs, gate_w, up_w, down_w, hidden, glu, slope, tile):
-    units, width = gate_w.shape
-    rows = hidden.shape[0]
-    wide = tile // CAP * MROWS
-    block = lambda cols: pl.BlockSpec((tile, cols), lambda i: (i, 0))
-    whole = pl.BlockSpec((units, width), lambda i: (0, 0))
-    packed = pl.BlockSpec((wide, MAIN), lambda i: (i, 0))
-    return pl.pallas_call(
-        backward_kernel,
-        grid=(rows // tile,),
-        in_specs=[packed, whole, whole, whole, block(units), block(units), block(units)],
-        out_specs=[block(width), block(units), block(units), packed],
-        out_shape=[
-            jax.ShapeDtypeStruct((rows, width), BF),
-            jax.ShapeDtypeStruct((rows, units), BF),
-            jax.ShapeDtypeStruct((rows, units), BF),
-            jax.ShapeDtypeStruct(msgs.shape, BF),
-        ],
-        scratch_shapes=[pltpu.VMEM((tile, MAIN + CHUNK), BF)],
-        compiler_params=pltpu.CompilerParams(vmem_limit_bytes=60 * 2**20),
-        cost_estimate=pl.CostEstimate(flops=6 * rows * width * units, bytes_accessed=30 * 2**20, transcendentals=0),
-    )(msgs, gate_w, up_w, down_w, hidden, glu, slope)
+        compiler_params=pltpu.CompilerParams(vmem_limit_bytes=62 * 2**20),
+        cost_estimate=pl.CostEstimate(flops=10 * rows * width * units, bytes_accessed=40 * 2**20, transcendentals=0),
+    )(rows_msg, wt_msg, gate_w, up_w, down_w)
 
 
 def combine_kernel(copies, expert_ref, slot_ref, prob_ref, back_ref, in_ref, prob_out_ref):
@@ -488,8 +513,7 @@
     rows_in, wt_in = exchange(table, rows_msg, cotangent.T)
     rows_in = rows_in.reshape(devices * MROWS, MAIN)
     wt_in = wt_in.reshape(devices * MROWS, MAIN)
-    rows, hidden, glu, slope = forward(rows_in, gate_w, up_w, 192)
-    weighted, gate_grad, up_grad, packed = backward(wt_in, gate_w, up_w, down_w, hidden, glu, slope, 192)
+    rows, weighted, hidden, gate_grad, up_grad, packed = expert(rows_in, wt_in, gate_w, up_w, down_w)
     back = lax.all_to_all(
         packed.reshape(devices, MROWS, MAIN), ("expert", "dp"), split_axis=0, concat_axis=0, tiled=True
     ).reshape(devices * MROWS, MAIN)

time: 220 us -> 209 us (0.950)
  Pallas kernels: 147 us -> 136 us
  matrix products: 20.9 us -> 18.3 us
  waiting for transfers between devices: 36.6 us -> 39.1 us
    pallas_call x2 -> x1, Pallas kernels: 47.9 us -> 36.8 us  [expert(): pl.pallas_call(expert_kernel, in_specs=[anywhere] * 5, out_specs=[anywher...]
    dot_general x1, matrix products: 7.85 us -> 5.23 us  [body(): lax.dot_general(weighted, hidden, contract_rows, preferred_element_type=F32)]
    all_to_all x1, waiting for transfers between devices: 36.6 us -> 39.1 us  [body(): lax.all_to_all(packed.reshape(devices, MROWS, MAIN), ('expert', 'dp'), sp...]
  transfers between devices with their start and end apart: 1 -> 1, of which waited for: 1 -> 1; matrix products, arithmetic and copies ran while one was open for 10% -> 9% of each run, Pallas kernels for 0% -> 0%
where the time goes in v3:
time: 209 us; the launch traced here: 208 us
  Pallas kernels  136 us (65%)
  waiting for transfers between devices  39.1 us (19%)
  matrix products  18.3 us (9%)
  starting transfers between devices  8.36 us (4%)
  local copies, waits for them, and re-layouts  4.48 us (2%)
    pallas_call x1, Pallas kernels, exchange(): pl.pallas_call(exchange_kernel, in_specs=[anywhere] * 3, out_specs=[anywh...  92.6 us
    all_to_all x1, waiting for transfers between devices, body(): lax.all_to_all(packed.reshape(devices, MROWS, MAIN), ('expert', 'dp'), sp...  39.1 us
    pallas_call x1, Pallas kernels, expert(): pl.pallas_call(expert_kernel, in_specs=[anywhere] * 5, out_specs=[anywher...  36.8 us
    all_to_all x1, starting transfers between devices, body(): lax.all_to_all(packed.reshape(devices, MROWS, MAIN), ('expert', 'dp'), sp...  8.36 us
    dot_general x1, matrix products, body(): lax.dot_general(rows, up_grad, contract_rows, preferred_element_type=F32)  7.85 us
    dot_general x1, matrix products, body(): lax.dot_general(rows, gate_grad, contract_rows, preferred_element_type=F32)  5.23 us
    dot_general x1, matrix products, body(): lax.dot_general(weighted, hidden, contract_rows, preferred_element_type=F32)  5.23 us
    pallas_call x1, Pallas kernels, combine(): pl.pallas_call(functools.partial(combine_kernel, copies), out_shape=(jax....  4.8 us
  transfers between devices with their start and end apart: 1, of which 1 were waited for; matrix products, arithmetic and copies ran while one was open for 9% of the time, Pallas kernels for 0%

profile of v3, /device:TPU:0, one launch (start us, length us, event | category | flops | bytes accessed | tf_op | source)
XLA Modules:
  0.0 208.2 jit_solution(4904325167301381636)
XLA Ops:
  0.6 0.7 convert_element_type.18
  1.3 0.1 copy.25
  1.5 0.1 copy.26
  1.5 0.7 fusion.3
  2.3 1.1 copy-done
  3.4 1.4 shard_map.119
  4.8 0.0 copy-start.1
  4.8 1.1 copy-done.1
  5.9 92.6 %shard_map.120 = (bf16[4,4,8,8,2304]{4,3,2,1,0:T(8,128)(2,1)}, bf16[4,4,8,8,2304]{4,3,2,1,0:T(8,128)(2,1)}) custom-call(f32[8,128]{1,0:T(8,128)S(1)} %pad_maximum_fusion.table_ref, bf16[4,4,4,8,2304]{4,3,2,1,0:T(8,128)(2,1)S(1)} %bitcast.33, bf16[2880,128]{1,0:T(8,128)(2,1)S(1)} %bitcast.35), custom_call_target="tpu_custom_call" | custom-call | tf_op jit(solution)/shard_map/pallas_call | solution.py:294
  98.6 36.8 %shard_map.121 = (bf16[768,2880]{1,0:T(8,128)(2,1)}, bf16[768,2880]{1,0:T(8,128)(2,1)}, bf16[768,720]{1,0:T(8,128)(2,1)}, bf16[768,720]{1,0:T(8,128)(2,1)}, bf16...) custom-call(bf16[1024,2304]{1,0:T(8,128)(2,1)} %bitcast.37, bf16[1024,2304]{1,0:T(8,128)(2,1)} %bitcast.38, ...), custom_call_target="tpu_custom_call" | custom-call | flops 15925248000 | bytes 41943040 | tf_op jit(solution)/shard_map/pallas_call | solution.py:435
  135.4 0.0 copy-start.2
  135.4 0.0 copy-start.3
  135.4 0.0 copy-start.7
  135.4 8.4 %all-to-all-start = ((bf16[128,8,2304]{2,1,0:T(8,128)(2,1)}), bf16[128,8,2304]{2,1,0:T(8,128)(2,1)}, u32[]{:S(2)}, u32[]{:S(2)}) async-start(bf16[128,8,2304]{2,1,0:T(8,128)(2,1)} %bitcast.36), calls=%async_computation | async-start | bytes 9437184 | tf_op jit(solution)/shard_map/all_to_all | solution.py:517
  143.8 0.1 copy.27.expert_ref
  143.9 0.1 copy.28.slot_ref
  144.1 0.0 copy-start.6
  144.1 7.8 %fusion.1 = bf16[1,2880,720]{1,2,0:T(8,128)(2,1)} fusion(bf16[768,2880]{1,0:T(8,128)(2,1)} %get-tuple-element.20, bf16[768,720]{1,0:T(8,128)(2,1)S(1)} %copy-done.7), kind=kOutput, calls=%fused_computation.4 | convolution fusion | flops 3187123200 | bytes 9676800 | tf_op jit(solution)/shard_map/dot_general | solution.py:523
  152.0 5.2 %fusion = bf16[1,2880,720]{1,2,0:T(8,128)(2,1)} fusion(bf16[768,2880]{1,0:T(8,128)(2,1)S(1)} %copy-done.4, bf16[768,720]{1,0:T(8,128)(2,1)S(1)} %copy-done.6), kind=kOutput, calls=%fused_computation.3 | convolution fusion | flops 3187123200 | bytes 9676800 | tf_op jit(solution)/shard_map/dot_general | solution.py:522
  157.2 5.2 %fusion.2 = bf16[1,2880,720]{1,2,0:T(8,128)(2,1)} fusion(bf16[768,2880]{1,0:T(8,128)(2,1)S(1)} %bitcast.43, bf16[768,720]{1,0:T(8,128)(2,1)S(1)} %copy-done.5), kind=kOutput, calls=%fused_computation.5 | convolution fusion | flops 3187123200 | bytes 9676800 | tf_op jit(solution)/shard_map/dot_general | solution.py:521
  162.4 39.1 %all-to-all-done = bf16[128,8,2304]{2,1,0:T(8,128)(2,1)} async-done(((bf16[128,8,2304]{2,1,0:T(8,128)(2,1)}), bf16[128,8,2304]{2,1,0:T(8,128)(2,1)}, u32[]{:S(2)}, u32[]{:S(2)}) %all-to-all-start) | async-done | bytes 4718624 | tf_op jit(solution)/shard_map/all_to_all | solution.py:517
  201.6 4.8 %shard_map.122 = (bf16[128,2880]{1,0:T(8,128)(2,1)S(1)}, f32[128,4]{1,0:T(8,128)S(1)}) custom-call(s32[128,4]{1,0:T(8,128)S(1)} %copy.27.expert_ref, s32[128,4]{1,0:T(8,128)S(1)} %copy.28.slot_ref, f32[128,4]{1,0:T(8,128)S(1)} %get-tuple-element.38.prob_ref, bf16[1024,2304]{1,0:T(8,128)(2,1)} %bitcast.14.back_ref), custom_call_target="tpu_custom_call" | custom-call | tf_op jit(solution)/shard_map/pallas_call | solution.py:493
  206.4 1.1 copy.29
  207.5 0.7 copy.30
  (16 shorter events, 0.1 us)
Async XLA Ops:
  2.3 1.1 copy-start
  4.8 1.1 copy-start.1
  135.4 8.4 %copy-start.2 = (s32[128,4]{0,1:T(4,128)S(1)}, s32[128,4]{0,1:T(4,128)}, u32[]{:S(2)}) copy-start(s32[128,4]{0,1:T(4,128)} %param.10) | copy-start | bytes 6148
  135.4 8.5 %copy-start.3 = (s32[128,4]{0,1:T(4,128)S(1)}, s32[128,4]{0,1:T(4,128)}, u32[]{:S(2)}) copy-start(s32[128,4]{0,1:T(4,128)} %param.11) | copy-start | bytes 6148
  135.4 8.6 %copy-start.7 = (bf16[768,720]{1,0:T(8,128)(2,1)S(1)}, bf16[768,720]{1,0:T(8,128)(2,1)}, u32[]{:S(2)}) copy-start(bf16[768,720]{1,0:T(8,128)(2,1)} %get-tuple-element.22) | copy-start | bytes 3317764
  135.4 66.1 %all-to-all-start = ((bf16[128,8,2304]{2,1,0:T(8,128)(2,1)}), bf16[128,8,2304]{2,1,0:T(8,128)(2,1)}, u32[]{:S(2)}, u32[]{:S(2)}) async-start(bf16[128,8,2304]{2,1,0:T(8,128)(2,1)} %bitcast.36), calls=%async_computation | async-start | bytes 9437184 | tf_op jit(solution)/shard_map/all_to_all | solution.py:517
  144.1 7.9 %copy-start.4 = (bf16[768,2880]{1,0:T(8,128)(2,1)S(1)}, bf16[768,2880]{1,0:T(8,128)(2,1)}, u32[]{:S(2)}) copy-start(bf16[768,2880]{1,0:T(8,128)(2,1)} %get-tuple-element.20) | copy-start | bytes 13271044
  144.1 7.9 %copy-start.6 = (bf16[768,720]{1,0:T(8,128)(2,1)S(1)}, bf16[768,720]{1,0:T(8,128)(2,1)}, u32[]{:S(2)}) copy-start(bf16[768,720]{1,0:T(8,128)(2,1)} %get-tuple-element.21) | copy-start | bytes 3317764
  144.1 13.1 %slice-start = ((s8[4521984]{0:T(1024)(128)(4,1)}), s8[4194304]{0:T(1024)(128)(4,1)S(1)}, s32[]{:S(2)}) async-start(s8[4521984]{0:T(1024)(128)(4,1)} %bitcast.42), calls=%async_computation.1 | async-start | bytes 8388608
  151.9 5.3 %slice-start.1 = ((s8[4521984]{0:T(1024)(128)(4,1)}), s8[327680]{0:T(1024)(128)(4,1)S(1)}, s32[]{:S(2)}) async-start(s8[4521984]{0:T(1024)(128)(4,1)} %bitcast.42), calls=%async_computation.2 | async-start | bytes 655360
  152.0 5.3 %copy-start.5 = (bf16[768,720]{1,0:T(8,128)(2,1)S(1)}, bf16[768,720]{1,0:T(8,128)(2,1)}, u32[]{:S(2)}) copy-start(bf16[768,720]{1,0:T(8,128)(2,1)} %get-tuple-element.24) | copy-start | bytes 3317764

commit v4 on v3

--- a/solution.py
+++ b/solution.py
@@ -12,8 +12,11 @@
 F32 = jnp.float32
 CAP = 6
 MROWS = 8
-MAIN = 2304
+MAIN = 2176
 CHUNK = 640
+ENDS = 64
+BODY = slice(MAIN, MAIN + CHUNK)
+LAST = slice(3 * CHUNK, MAIN)
 
 
 def dot(a, b):
@@ -34,9 +37,15 @@
     row = iota((total, 1), 0)
     slot = row % MROWS
     message = row // MROWS
-    rem_ref[...] = jnp.zeros_like(rem_ref)
-    rem_ref[: width - MAIN, :] = tok_ref[MAIN:, :]
+    set_ends(rem_ref, tok_ref)
     place_into(rows_ref, message, slot, [(code_ref[k : k + 1, :], None) for k in range(code_ref.shape[0])], tok_ref, rem_ref)
+
+
+def set_ends(ends, src):
+    toks = src.shape[1]
+    ends[...] = jnp.zeros_like(ends)
+    for j in range(3):
+        ends[j * ENDS : (j + 1) * ENDS, j * toks : (j + 1) * toks] = src[MAIN + CHUNK :, :]
 
 
 def place_into(dst, expert, slot, choices, src, rest):
@@ -50,11 +59,13 @@
         return out.astype(BF)
 
     main = matrix(jnp.where(slot < CAP, expert * MROWS + slot, -2).astype(code_type(choices)))
+    extras = []
     for j in range(3):
         cols = slice(j * CHUNK, (j + 1) * CHUNK)
-        extra = matrix(jnp.where(slot >= CAP, expert * MROWS + 3 * (slot - CAP) + j, -2).astype(code_type(choices)))
-        dst[:, cols] = (dot_nt(main, src[cols, :]) + dot_nt(extra, rest[...])).astype(BF)
-    dst[:, 3 * CHUNK :] = dot_nt(main, src[3 * CHUNK : MAIN, :]).astype(BF)
+        wanted = jnp.where(slot >= CAP, expert * MROWS + 3 * (slot - CAP) + j, -2)
+        extras.append(matrix(wanted.astype(code_type(choices))))
+        dst[:, cols] = (dot_nt(main, src[cols, :]) + dot_nt(extras[j], src[BODY, :])).astype(BF)
+    dst[:, LAST] = (dot_nt(main, src[LAST, :]) + dot_nt(jnp.concatenate(extras, axis=1), rest[...])).astype(BF)
 
 
 def code_type(choices):
@@ -65,7 +76,7 @@
     return pl.pallas_call(
         pack_kernel,
         out_shape=jax.ShapeDtypeStruct((experts * MROWS, MAIN), BF),
-        scratch_shapes=[pltpu.VMEM((CHUNK, tokens_t.shape[1]), BF)],
+        scratch_shapes=[pltpu.VMEM((MAIN - 3 * CHUNK, 3 * tokens_t.shape[1]), BF)],
         compiler_params=pltpu.CompilerParams(vmem_limit_bytes=40 * 2**20),
     )(code, tokens_t)
 
@@ -73,14 +84,15 @@
 STEPS = (1, 3, 2)
 LINE = ((1, 0), (3, 0), (2, 0), (1, 1), (3, 1), (2, 1), (0, 1))
 MESH = pl.DeviceIdType.MESH
-HALF = MAIN // 2
-PARTS = 2
-BLOCKS = 8 // PARTS
+WIDTHS = (1152, MAIN - 1152)
+PARTS = 4
+EARLY = True
 
 
 def exchange_kernel(table_ref, rows_ref, cot_ref, rows_out, wt_out, *scratch):
-    (relay_a, held_a, relay_b, cots, tables, sent, rest, block_buf) = scratch[:8]
-    (tab_s, tab_r, cot_s, cot_r, a1_s, a1_r, a2_s, a2_r, a3_s, a3_r, b1_s, b1_r, b2_s, b2_r, own) = scratch[8:]
+    relay_a, held_a, relay_b = scratch[:2], scratch[2:4], scratch[4:6]
+    (cots, tables, sent, rest, block_buf) = scratch[6:11]
+    (tab_s, tab_r, cot_s, cot_r, a1_s, a1_r, a2_s, a2_r, a3_s, a3_r, b1_s, b1_r, b2_s, b2_r, own) = scratch[11:]
     e, d = lax.axis_index("expert"), lax.axis_index("dp")
     z, y, x, c = e // 16, (e // 4) % 4, d * 2 + (e // 2) % 2, e % 2
     xc, sub = x * 2 + c, (x % 2) * 2 + c
@@ -116,7 +128,7 @@
         return copy
 
     mine = (z, y)
-    halves = (pl.ds(0, HALF), pl.ds(HALF, HALF))
+    halves = (pl.ds(0, WIDTHS[0]), pl.ds(*WIDTHS))
 
     def at(h, first, second):
         return (first, second) if h == 0 else (second, first)
@@ -137,7 +149,7 @@
     a1 = [[None] * 3, [None] * 3]
     a2 = [[[None] * 3 for _ in range(4)] for _ in range(2)]
     for h in range(2):
-        keep(rows_ref.at[z, y, :, :, halves[h]], relay_a.at[h, mine[h], mine[1 - h]], own.at[2 + h])
+        keep(rows_ref.at[z, y, :, :, halves[h]], relay_a[h].at[mine[h], mine[1 - h]], own.at[2 + h])
     for i, off in enumerate(LINE):
         tab = send(table_ref, tables.at[xc], tab_s.at[i], tab_r.at[i], device(0, 0, *off))
     tab_copies = started[-len(LINE) :]
@@ -153,7 +165,7 @@
             to = (mine[h] + step) % 4
             a1[h][i] = send(
                 pick(rows_ref, h, to, every, every, every, halves[h]),
-                relay_a.at[h, mine[h]],
+                relay_a[h].at[mine[h]],
                 a1_s.at[h, i],
                 a1_r.at[h, i],
                 first_step(h, step),
@@ -167,30 +179,17 @@
                 src = pick(rows_ref, h, mine[h], to, every, every, halves[h])
                 place = mine[h]
             else:
-                src = relay_a.at[h, source, to]
+                src = relay_a[h].at[source, to]
                 place = source
-            a2[h][i][j] = send(src, held_a.at[h, mine[1 - h], place], a2_s.at[h, i, j], a2_r.at[h, i, j], second_step(h, step))
+            a2[h][i][j] = send(src, held_a[h].at[mine[1 - h], place], a2_s.at[h, i, j], a2_r.at[h, i, j], second_step(h, step))
 
     for h in range(2):
         forward_rows(h, 3, None)
+
     def forward_a1(i):
         for h in range(2):
             a1[h][i].wait_recv()
             forward_rows(h, i, (mine[h] - STEPS[i]) % 4)
-
-    forward_a1(0)
-    forward_a1(1)
-    far = []
-    for i, step in enumerate((1, 3)):
-        block = ((x - step) % 4) * 2 + c
-        near[i].wait_recv()
-        far.append(send_cot(cots.at[block, parts[i]], cots.at[block, parts[i]], 2 + i, device(0, 0, step)))
-        other_core.append(send_cot(cots.at[block], cots.at[block], 5 + i, device(0, 0, 0, 1)))
-    forward_a1(2)
-    block = ((x + 2) % 4) * 2 + c
-    for i in range(2):
-        far[i].wait_recv()
-        other_core.append(send_cot(cots.at[block, parts[i]], cots.at[block, parts[i]], 7 + i, device(0, 0, 0, 1)))
 
     def spread_rows(h, group, source, place):
         where = pick(rows_out, h, every, place, xc, every, halves[h])
@@ -205,35 +204,29 @@
             )
         keep(source.at[:, sub], where, own.at[4 + 4 * h + group])
 
-    for copy in local[:4]:
-        copy.wait()
-    for h in range(2):
-        spread_rows(h, 3, relay_a.at[h, :, mine[1 - h]], mine[1 - h])
-
-    rest[...] = jnp.zeros_like(rest)
-    width = cot_ref.shape[0]
     row = iota((16 * MROWS, 1), 0)
 
     def make_block(b):
-        rest[: width - MAIN, :] = cots[b, MAIN:, :]
+        set_ends(rest, cots.at[b])
         choices = [(tables[b, k : k + 1, :], tables[b, 4 + k : 5 + k, :]) for k in range(4)]
         place_into(block_buf, (row // MROWS) * 4 + sub, row % MROWS, choices, cots.at[b], rest)
         sent[:, :, b] = block_buf[...].reshape(4, 4, MROWS, MAIN)
 
-    for copy in tab_copies + other_core:
-        copy.wait_recv()
-    b1 = [[[None] * 3, [None] * 3] for _ in range(PARTS)]
-    b2 = [[[[None] * 3 for _ in range(4)] for _ in range(2)] for _ in range(PARTS)]
+    b1 = [[[None] * 3, [None] * 3] for _ in range(4)]
+    b2 = [[[[None] * 3 for _ in range(4)] for _ in range(2)] for _ in range(4)]
+
+    def blocks_of(p):
+        return pl.ds(((x - (0, 1, 3, 2)[p]) % 4) * 2, 2)
 
     def forward_wts(p, h, i, source):
-        blocks = pl.ds(p * BLOCKS, BLOCKS)
+        blocks = blocks_of(p)
         for j, step in enumerate(STEPS + (0,)):
             to = (mine[1 - h] + step) % 4
             if source is None:
                 src = pick(sent, h, mine[h], to, blocks, every, halves[h])
                 place = mine[h]
             else:
-                src = relay_b.at[h, source, to, blocks]
+                src = relay_b[h].at[source, to, blocks]
                 place = source
             dst = pick(wt_out, h, place, mine[1 - h], blocks, every, halves[h])
             if step:
@@ -241,19 +234,19 @@
             else:
                 keep(src, dst, own.at[12 + (p * 2 + h) * 4 + i])
 
-    for p in range(PARTS):
-        blocks = pl.ds(p * BLOCKS, BLOCKS)
-
-        @pl.loop(p * BLOCKS, (p + 1) * BLOCKS)
+    def send_part(p):
+        start = ((x - (0, 1, 3, 2)[p]) % 4) * 2
+
+        @pl.loop(0, 2)
         def _(b):
-            make_block(b)
+            make_block(start + b)
 
         for i, step in enumerate(STEPS):
             for h in range(2):
                 to = (mine[h] + step) % 4
                 b1[p][h][i] = send(
-                    pick(sent, h, to, every, blocks, every, halves[h]),
-                    relay_b.at[h, mine[h], :, blocks],
+                    pick(sent, h, to, every, blocks_of(p), every, halves[h]),
+                    relay_b[h].at[mine[h], :, blocks_of(p)],
                     b1_s.at[p, h, i],
                     b1_r.at[p, h, i],
                     first_step(h, step),
@@ -261,18 +254,52 @@
         for h in range(2):
             forward_wts(p, h, 3, None)
 
+    def relay_part(p):
+        for i, step in enumerate(STEPS):
+            for h in range(2):
+                b1[p][h][i].wait_recv()
+                forward_wts(p, h, i, (mine[h] - step) % 4)
+
+    for copy in local[:4]:
+        copy.wait()
+    for copy in tab_copies:
+        copy.wait_recv()
+    other_core[0].wait_recv()
+    if EARLY:
+        send_part(0)
+    forward_a1(0)
+    forward_a1(1)
+    far = []
+    for i, step in enumerate((1, 3)):
+        block = ((x - step) % 4) * 2 + c
+        near[i].wait_recv()
+        far.append(send_cot(cots.at[block, parts[i]], cots.at[block, parts[i]], 2 + i, device(0, 0, step)))
+        other_core.append(send_cot(cots.at[block], cots.at[block], 5 + i, device(0, 0, 0, 1)))
+    forward_a1(2)
+    for h in range(2):
+        spread_rows(h, 3, relay_a[h].at[:, mine[1 - h]], mine[1 - h])
+    if not EARLY:
+        send_part(0)
+    for p in (1, 2):
+        other_core[p].wait_recv()
+        send_part(p)
+    block = ((x + 2) % 4) * 2 + c
+    for i in range(2):
+        far[i].wait_recv()
+        other_core.append(send_cot(cots.at[block, parts[i]], cots.at[block, parts[i]], 7 + i, device(0, 0, 0, 1)))
+    for copy in other_core[3:]:
+        copy.wait_recv()
+    send_part(3)
+    if EARLY:
+        relay_part(0)
     for j, step in enumerate(STEPS):
         for h in range(2):
             for i in range(4):
                 a2[h][i][j].wait_recv()
             place = (mine[1 - h] - step) % 4
-            spread_rows(h, j, held_a.at[h, place], place)
-
-    for p in range(PARTS):
-        for i, step in enumerate(STEPS):
-            for h in range(2):
-                b1[p][h][i].wait_recv()
-                forward_wts(p, h, i, (mine[h] - step) % 4)
+            spread_rows(h, j, held_a[h].at[place], place)
+    for p in range(1 if EARLY else 0, 4):
+        relay_part(p)
 
     early = {id(copy) for copy in tab_copies + near + far + other_core}
     for group in a1 + [v for half in a2 for v in half] + [v for part in b1 for v in part]:
@@ -297,18 +324,16 @@
         out_specs=[anywhere] * 2,
         out_shape=[out, out],
         scratch_shapes=[
-            pltpu.VMEM((2, 4, 4, 4, MROWS, HALF), BF),
-            pltpu.VMEM((2, 4, 4, 4, MROWS, HALF), BF),
-            pltpu.VMEM((2, 4, 4, 8, MROWS, HALF), BF),
+            *[pltpu.VMEM((4, 4, at, MROWS, half), BF) for at in (4, 4, 8) for half in WIDTHS],
             pltpu.VMEM((8, *cot_t.shape), BF),
             pltpu.VMEM((8, *table.shape), F32),
             pltpu.VMEM((4, 4, 8, MROWS, MAIN), BF),
-            pltpu.VMEM((CHUNK, cot_t.shape[1]), BF),
+            pltpu.VMEM((MAIN - 3 * CHUNK, 3 * cot_t.shape[1]), BF),
             pltpu.VMEM((16 * MROWS, MAIN), BF),
             *sems,
             pltpu.SemaphoreType.DMA((12 + 8 * PARTS,)),
         ],
-        compiler_params=pltpu.CompilerParams(collective_id=0, has_side_effects=True, vmem_limit_bytes=48 * 2**20),
+        compiler_params=pltpu.CompilerParams(collective_id=0, has_side_effects=True, vmem_limit_bytes=62 * 2**20),
     )(table, rows_msg.reshape(4, 4, 4, MROWS, MAIN), cot_t)
 
 
@@ -342,7 +367,6 @@
     arrive, leave = sems
     total, width = rows.shape
     tiles = total // TILE
-    rest = width - MAIN
 
     def tile_of(i, size):
         return pl.ds(pl.multiple_of(i * size, size), size)
@@ -369,10 +393,13 @@
         def _(i):
             wide, tile = tile_of(i, WIDE), tile_of(i, TILE)
             dst[tile, :MAIN] = dot(main, src[wide, :MAIN]).astype(BF)
-            part = dot(rem[0], src[wide, :rest])
+            part = dot(rem[0], src[wide, :CHUNK])
             for j in (1, 2):
-                part = part + dot(rem[j], src[wide, j * CHUNK : j * CHUNK + rest])
-            dst[tile, MAIN:] = part.astype(BF)
+                part = part + dot(rem[j], src[wide, j * CHUNK : (j + 1) * CHUNK])
+            dst[tile, BODY] = part.astype(BF)
+            one, two = src[wide, 3 * CHUNK : 3 * CHUNK + 128], src[wide, 3 * CHUNK + 128 :]
+            ends = dot(rem[0], one) + pltpu.roll(dot(rem[1], one), ENDS, 1) + dot(rem[2], two)
+            dst[tile, MAIN + CHUNK :] = ends[:, :ENDS].astype(BF)
 
     got_rows.wait()
     unpack(msg_rows, rows)
@@ -398,9 +425,10 @@
     puts.append(put(2, weighted, weighted_out))
     got_down.wait()
     main_t, rem_t, last_t = picks(WIDE, TILE, True, True)
-    spare = MAIN - 3 * CHUNK
-    lane = iota((TILE, spare), 1)
-    spot = 2 * ((iota((TILE, spare), 0) % CAP) % 3)
+    lane = iota((TILE, 128), 1)
+    slot = iota((TILE, 128), 0) % CAP
+    which = slot % 3
+    spot = ENDS + 2 * which
     hgrad = dot_nt(weighted[...], down_w[...])
     share = jnp.sum(hgrad * hidden[...].astype(F32), axis=1, keepdims=True)
     up_grad[...] = (hgrad * glu[...]).astype(BF)
@@ -413,15 +441,18 @@
         full[:, cols] = (dot(gate_grad[...], gate_w[:, cols]) + dot(up_grad[...], up_w[:, cols])).astype(BF)
     for i in range(tiles):
         tile, wide = slice(i * TILE, (i + 1) * TILE), slice(i * WIDE, (i + 1) * WIDE)
-        tail = full[tile, MAIN : MAIN + CHUNK]
         for j in range(3):
             cols = slice(j * CHUNK, (j + 1) * CHUNK)
-            msg_wt[wide, cols] = (dot(main_t, full[tile, cols]) + dot(rem_t[j], tail)).astype(BF)
+            msg_wt[wide, cols] = (dot(main_t, full[tile, cols]) + dot(rem_t[j], full[tile, BODY])).astype(BF)
         part = share[tile, :]
         head = part.astype(BF).astype(F32)
-        pair = jnp.where(lane == spot, head, jnp.where(lane == spot + 1, part - head, 0.0)).astype(BF)
-        cols = slice(3 * CHUNK, MAIN)
-        msg_wt[wide, cols] = (dot(main_t, full[tile, cols]) + dot(last_t, pair)).astype(BF)
+        pair = jnp.where(lane == spot, head, jnp.where(lane == spot + 1, part - head, 0.0))
+        ends = full[tile, MAIN + CHUNK :].astype(F32)
+        one = jnp.where(which == 0, ends, jnp.where(which == 1, pltpu.roll(ends, ENDS, 1), 0.0))
+        two = jnp.where(which == 2, ends, 0.0) + pair
+        for k, value in enumerate((one, two)):
+            cols = slice(3 * CHUNK + 128 * k, 3 * CHUNK + 128 * (k + 1))
+            msg_wt[wide, cols] = (dot(main_t, full[tile, cols]) + dot(last_t, value.astype(BF))).astype(BF)
         puts.append(put(5 + i, msg_wt.at[wide], packed_out.at[wide]))
     for copy in puts:
         copy.wait()
@@ -443,7 +474,7 @@
             *[pltpu.VMEM(wide, BF)] * 2,
             *[pltpu.VMEM(thin, BF)] * 3,
             *[pltpu.VMEM(thin, F32)] * 2,
-            pltpu.VMEM((rows, MAIN + CHUNK), BF),
+            pltpu.VMEM((rows, MAIN + CHUNK + 128), BF),
             pltpu.SemaphoreType.DMA((5,)),
             pltpu.SemaphoreType.DMA((5 + rows // TILE,)),
         ],
@@ -453,7 +484,7 @@
 
 
 def combine_kernel(copies, expert_ref, slot_ref, prob_ref, back_ref, in_ref, prob_out_ref):
-    toks, rest = in_ref.shape[0], in_ref.shape[1] - MAIN
+    toks = in_ref.shape[0]
     total = back_ref.shape[0]
     col = iota((toks, total), 1)
     message = col // MROWS
@@ -463,7 +494,7 @@
     main, rem = zero, [zero] * 3
     sums = []
     lane = iota((toks, 128), 1)
-    shares = back_ref[:, 3 * CHUNK : 3 * CHUNK + 128]
+    first, shares = back_ref[:, 3 * CHUNK : 3 * CHUNK + 128], back_ref[:, 3 * CHUNK + 128 :]
     for k in range(expert_ref.shape[1]):
         expert, slot = expert_ref[:, k : k + 1], slot_ref[:, k : k + 1]
         kept = slot >= 0
@@ -475,13 +506,17 @@
         for j in range(3):
             rem[j] = jnp.where(tail & (which == j), 1.0, rem[j])
         got = dot(jnp.where(tail, 1.0, 0.0).astype(BF), shares)
-        got = jnp.where((lane == 2 * which) | (lane == 2 * which + 1), got, 0.0)
+        spot = ENDS + 2 * which
+        got = jnp.where((lane == spot) | (lane == spot + 1), got, 0.0)
         sums.append(jnp.sum(got, axis=1, keepdims=True))
     in_ref[:, :MAIN] = dot(main.astype(BF), back_ref[...]).astype(BF)
-    part = dot(rem[0].astype(BF), back_ref[:, :rest])
+    rem = [value.astype(BF) for value in rem]
+    part = dot(rem[0], back_ref[:, :CHUNK])
     for j in (1, 2):
-        part = part + dot(rem[j].astype(BF), back_ref[:, j * CHUNK : j * CHUNK + rest])
-    in_ref[:, MAIN:] = part.astype(BF)
+        part = part + dot(rem[j], back_ref[:, j * CHUNK : (j + 1) * CHUNK])
+    in_ref[:, BODY] = part.astype(BF)
+    ends = dot(rem[0], first) + pltpu.roll(dot(rem[1], first), ENDS, 1) + dot(rem[2], shares)
+    in_ref[:, MAIN + CHUNK :] = ends[:, :ENDS].astype(BF)
     choice = iota(prob_ref.shape, 1)
     total_share = jnp.zeros(prob_ref.shape, F32)
     for k, value in enumerate(sums):

time: 209 us -> 200 us (0.957)
  Pallas kernels: 136 us -> 129 us
  waiting for transfers between devices: 39.1 us -> 36.2 us
    pallas_call x1, Pallas kernels: 92.6 us -> 84.9 us  [exchange(): pl.pallas_call(exchange_kernel, in_specs=[anywhere] * 3, out_specs=[anywh...]
    all_to_all x1, waiting for transfers between devices: 39.1 us -> 36.2 us  [body(): lax.all_to_all(packed.reshape(devices, MROWS, MAIN), ('expert', 'dp'), sp...]
where the time goes in v4:
time: 200 us
  Pallas kernels  129 us (64%)
  waiting for transfers between devices  36.2 us (18%)
  matrix products  18.3 us (9%)
  starting transfers between devices  9.39 us (5%)
  local copies, waits for them, and re-layouts  4.73 us (2%)
  other arithmetic  2.02 us (1%)
    pallas_call x1, Pallas kernels, exchange(): pl.pallas_call(exchange_kernel, in_specs=[anywhere] * 3, out_specs=[anywh...  84.9 us
    pallas_call x1, Pallas kernels, expert(): pl.pallas_call(expert_kernel, in_specs=[anywhere] * 5, out_specs=[anywher...  37.2 us
    all_to_all x1, waiting for transfers between devices, body(): lax.all_to_all(packed.reshape(devices, MROWS, MAIN), ('expert', 'dp'), sp...  36.2 us
    all_to_all x1, starting transfers between devices, body(): lax.all_to_all(packed.reshape(devices, MROWS, MAIN), ('expert', 'dp'), sp...  9.39 us
    dot_general x1, matrix products, body(): lax.dot_general(rows, up_grad, contract_rows, preferred_element_type=F32)  7.85 us
    dot_general x1, matrix products, body(): lax.dot_general(rows, gate_grad, contract_rows, preferred_element_type=F32)  5.23 us
    dot_general x1, matrix products, body(): lax.dot_general(weighted, hidden, contract_rows, preferred_element_type=F32)  5.23 us
    pallas_call x1, Pallas kernels, combine(): pl.pallas_call(functools.partial(combine_kernel, copies), out_shape=(jax....  4.95 us
  transfers between devices with their start and end apart: 1, of which 1 were waited for; matrix products, arithmetic and copies ran while one was open for 9% of the time, Pallas kernels for 0%

profile of v4, /device:TPU:0, one launch (start us, length us, event | category | flops | bytes accessed | tf_op | source)
XLA Modules:
  0.0 199.9 jit_solution(2172484563707487751)
XLA Ops:
  0.6 0.7 convert_element_type.18
  1.3 0.1 copy.25
  1.5 0.1 copy.26
  1.5 0.7 fusion.3
  2.3 0.6 pad_maximum_fusion.table_ref
  2.9 1.1 copy-done.1
  4.0 1.5 shard_map.119
  5.5 0.0 copy-start
  5.5 1.4 copy-done
  6.9 84.9 %shard_map.120 = (bf16[4,4,8,8,2176]{4,3,2,1,0:T(8,128)(2,1)}, bf16[4,4,8,8,2176]{4,3,2,1,0:T(8,128)(2,1)}) custom-call(f32[8,128]{1,0:T(8,128)} %pad_maximum_fusion.table_ref, bf16[4,4,4,8,2176]{4,3,2,1,0:T(8,128)(2,1)} %bitcast.33, bf16[2880,128]{1,0:T(8,128)(2,1)} %bitcast.36), custom_call_target="tpu_custom_call" | custom-call | tf_op jit(solution)/shard_map/pallas_call | solution.py:321
  91.7 37.2 %shard_map.121 = (bf16[768,2880]{1,0:T(8,128)(2,1)}, bf16[768,2880]{1,0:T(8,128)(2,1)}, bf16[768,720]{1,0:T(8,128)(2,1)}, bf16[768,720]{1,0:T(8,128)(2,1)}, bf16...) custom-call(bf16[1024,2176]{1,0:T(8,128)(2,1)} %bitcast.37, bf16[1024,2176]{1,0:T(8,128)(2,1)} %bitcast.38, ...), custom_call_target="tpu_custom_call" | custom-call | flops 15925248000 | bytes 41943040 | tf_op jit(solution)/shard_map/pallas_call | solution.py:466
  128.9 0.0 copy-start.2
  129.0 0.0 copy-start.3
  129.0 0.0 copy-start.7
  129.0 9.4 %all-to-all-start = ((bf16[128,8,2176]{2,1,0:T(8,128)(2,1)}), bf16[128,8,2176]{2,1,0:T(8,128)(2,1)}, u32[]{:S(2)}, u32[]{:S(2)}) async-start(bf16[128,8,2176]{2,1,0:T(8,128)(2,1)} %bitcast.35), calls=%async_computation | async-start | bytes 8912896 | tf_op jit(solution)/shard_map/all_to_all | solution.py:552
  138.4 0.1 copy.27.expert_ref
  138.5 0.1 copy.28.slot_ref
  138.7 7.8 %fusion.1 = bf16[1,2880,720]{1,2,0:T(8,128)(2,1)} fusion(bf16[768,2880]{1,0:T(8,128)(2,1)} %get-tuple-element.20, bf16[768,720]{1,0:T(8,128)(2,1)S(1)} %copy-done.7), kind=kOutput, calls=%fused_computation.4 | convolution fusion | flops 3187123200 | bytes 9676800 | tf_op jit(solution)/shard_map/dot_general | solution.py:558
  146.5 5.2 %fusion = bf16[1,2880,720]{1,2,0:T(8,128)(2,1)} fusion(bf16[768,2880]{1,0:T(8,128)(2,1)S(1)} %copy-done.4, bf16[768,720]{1,0:T(8,128)(2,1)S(1)} %copy-done.6), kind=kOutput, calls=%fused_computation.3 | convolution fusion | flops 3187123200 | bytes 9676800 | tf_op jit(solution)/shard_map/dot_general | solution.py:557
  151.8 5.2 %fusion.2 = bf16[1,2880,720]{1,2,0:T(8,128)(2,1)} fusion(bf16[768,2880]{1,0:T(8,128)(2,1)S(1)} %bitcast.43, bf16[768,720]{1,0:T(8,128)(2,1)S(1)} %copy-done.5), kind=kOutput, calls=%fused_computation.5 | convolution fusion | flops 3187123200 | bytes 9676800 | tf_op jit(solution)/shard_map/dot_general | solution.py:556
  157.0 36.2 %all-to-all-done = bf16[128,8,2176]{2,1,0:T(8,128)(2,1)} async-done(((bf16[128,8,2176]{2,1,0:T(8,128)(2,1)}), bf16[128,8,2176]{2,1,0:T(8,128)(2,1)}, u32[]{:S(2)}, u32[]{:S(2)}) %all-to-all-start) | async-done | bytes 4456480 | tf_op jit(solution)/shard_map/all_to_all | solution.py:552
  193.2 4.9 %shard_map.122 = (bf16[128,2880]{1,0:T(8,128)(2,1)S(1)}, f32[128,4]{1,0:T(8,128)S(1)}) custom-call(s32[128,4]{1,0:T(8,128)S(1)} %copy.27.expert_ref, s32[128,4]{1,0:T(8,128)S(1)} %copy.28.slot_ref, f32[128,4]{1,0:T(8,128)S(1)} %get-tuple-element.38.prob_ref, bf16[1024,2176]{1,0:T(8,128)(2,1)} %bitcast.14.back_ref), custom_call_target="tpu_custom_call" | custom-call | tf_op jit(solution)/shard_map/pallas_call | solution.py:528
  198.1 1.1 copy.29
  199.3 0.7 copy.30
  (16 shorter events, 0.0 us)
Async XLA Ops:
  2.9 1.1 copy-start.1
  5.5 1.4 copy-start
  128.9 9.4 %copy-start.2 = (s32[128,4]{0,1:T(4,128)S(1)}, s32[128,4]{0,1:T(4,128)}, u32[]{:S(2)}) copy-start(s32[128,4]{0,1:T(4,128)} %param.10) | copy-start | bytes 6148
  129.0 9.6 %copy-start.3 = (s32[128,4]{0,1:T(4,128)S(1)}, s32[128,4]{0,1:T(4,128)}, u32[]{:S(2)}) copy-start(s32[128,4]{0,1:T(4,128)} %param.11) | copy-start | bytes 6148
  129.0 9.7 %copy-start.7 = (bf16[768,720]{1,0:T(8,128)(2,1)S(1)}, bf16[768,720]{1,0:T(8,128)(2,1)}, u32[]{:S(2)}) copy-start(bf16[768,720]{1,0:T(8,128)(2,1)} %get-tuple-element.22) | copy-start | bytes 3317764
  129.0 64.2 %all-to-all-start = ((bf16[128,8,2176]{2,1,0:T(8,128)(2,1)}), bf16[128,8,2176]{2,1,0:T(8,128)(2,1)}, u32[]{:S(2)}, u32[]{:S(2)}) async-start(bf16[128,8,2176]{2,1,0:T(8,128)(2,1)} %bitcast.35), calls=%async_computation | async-start | bytes 8912896 | tf_op jit(solution)/shard_map/all_to_all | solution.py:552
  138.6 7.9 %copy-start.4 = (bf16[768,2880]{1,0:T(8,128)(2,1)S(1)}, bf16[768,2880]{1,0:T(8,128)(2,1)}, u32[]{:S(2)}) copy-start(bf16[768,2880]{1,0:T(8,128)(2,1)} %get-tuple-element.20) | copy-start | bytes 13271044
  138.6 7.9 %copy-start.6 = (bf16[768,720]{1,0:T(8,128)(2,1)S(1)}, bf16[768,720]{1,0:T(8,128)(2,1)}, u32[]{:S(2)}) copy-start(bf16[768,720]{1,0:T(8,128)(2,1)} %get-tuple-element.21) | copy-start | bytes 3317764
  138.7 13.1 %slice-start = ((s8[4521984]{0:T(1024)(128)(4,1)}), s8[4194304]{0:T(1024)(128)(4,1)S(1)}, s32[]{:S(2)}) async-start(s8[4521984]{0:T(1024)(128)(4,1)} %bitcast.42), calls=%async_computation.1 | async-start | bytes 8388608
  146.5 5.3 %slice-start.1 = ((s8[4521984]{0:T(1024)(128)(4,1)}), s8[327680]{0:T(1024)(128)(4,1)S(1)}, s32[]{:S(2)}) async-start(s8[4521984]{0:T(1024)(128)(4,1)} %bitcast.42), calls=%async_computation.2 | async-start | bytes 655360
  146.5 5.3 %copy-start.5 = (bf16[768,720]{1,0:T(8,128)(2,1)S(1)}, bf16[768,720]{1,0:T(8,128)(2,1)}, u32[]{:S(2)}) copy-start(bf16[768,720]{1,0:T(8,128)(2,1)} %get-tuple-element.24) | copy-start | bytes 3317764

commit v5 on v4

--- a/solution.py
+++ b/solution.py
@@ -31,14 +31,17 @@
     return lax.broadcasted_iota(jnp.int32, shape, dim)
 
 
-def pack_kernel(code_ref, tok_ref, rows_ref, rem_ref):
-    width, toks = tok_ref.shape
+def pack_kernel(expert_ref, slot_ref, prob_ref, tok_ref, rows_ref, table_ref, rem_ref):
+    top = expert_ref.shape[0]
+    code = jnp.where(slot_ref[...] >= 0, expert_ref[...] * MROWS + slot_ref[...], -1)
+    table_ref[:top, :] = code.astype(F32)
+    table_ref[top:, :] = prob_ref[...].astype(BF).astype(F32)
     total = rows_ref.shape[0]
     row = iota((total, 1), 0)
     slot = row % MROWS
     message = row // MROWS
     set_ends(rem_ref, tok_ref)
-    place_into(rows_ref, message, slot, [(code_ref[k : k + 1, :], None) for k in range(code_ref.shape[0])], tok_ref, rem_ref)
+    place_into(rows_ref, message, slot, [(code[k : k + 1, :], None) for k in range(top)], tok_ref, rem_ref)
 
 
 def set_ends(ends, src):
@@ -72,13 +75,16 @@
     return choices[0][0].dtype
 
 
-def pack(code, tokens_t, experts):
+def pack(expert_t, slot_t, prob_t, tokens_t, experts):
     return pl.pallas_call(
         pack_kernel,
-        out_shape=jax.ShapeDtypeStruct((experts * MROWS, MAIN), BF),
+        out_shape=(
+            jax.ShapeDtypeStruct((experts * MROWS, MAIN), BF),
+            jax.ShapeDtypeStruct((2 * slot_t.shape[0], slot_t.shape[1]), F32),
+        ),
         scratch_shapes=[pltpu.VMEM((MAIN - 3 * CHUNK, 3 * tokens_t.shape[1]), BF)],
-        compiler_params=pltpu.CompilerParams(vmem_limit_bytes=40 * 2**20),
-    )(code, tokens_t)
+        compiler_params=pltpu.CompilerParams(vmem_limit_bytes=67_043_328),
+    )(expert_t, slot_t, prob_t, tokens_t)
 
 
 STEPS = (1, 3, 2)
@@ -333,7 +339,7 @@
             *sems,
             pltpu.SemaphoreType.DMA((12 + 8 * PARTS,)),
         ],
-        compiler_params=pltpu.CompilerParams(collective_id=0, has_side_effects=True, vmem_limit_bytes=62 * 2**20),
+        compiler_params=pltpu.CompilerParams(collective_id=0, has_side_effects=True, vmem_limit_bytes=67_043_328),
     )(table, rows_msg.reshape(4, 4, 4, MROWS, MAIN), cot_t)
 
 
@@ -362,7 +368,7 @@
 
 def expert_kernel(rows_msg, wt_msg, gate_hbm, up_hbm, down_hbm, *refs):
     outs, bufs, sems = refs[:6], refs[6:-2], refs[-2:]
-    msg_rows, msg_wt, gate_w, up_w, down_w, rows, weighted, hidden, gate_grad, up_grad, glu, slope, full = bufs
+    msg_rows, msg_wt, gate_w, up_w, down_w, rows, weighted, hidden, gate_grad, up_grad, glu, slope, full, shares = bufs
     rows_out, weighted_out, hidden_out, gate_grad_out, up_grad_out, packed_out = outs
     arrive, leave = sems
     total, width = rows.shape
@@ -439,12 +445,15 @@
     for start in range(0, width, 768):
         cols = slice(start, min(width, start + 768))
         full[:, cols] = (dot(gate_grad[...], gate_w[:, cols]) + dot(up_grad[...], up_w[:, cols])).astype(BF)
-    for i in range(tiles):
-        tile, wide = slice(i * TILE, (i + 1) * TILE), slice(i * WIDE, (i + 1) * WIDE)
+    shares[...] = jnp.broadcast_to(share, shares.shape)
+
+    @pl.loop(0, tiles)
+    def _(i):
+        tile, wide = tile_of(i, TILE), tile_of(i, WIDE)
         for j in range(3):
             cols = slice(j * CHUNK, (j + 1) * CHUNK)
             msg_wt[wide, cols] = (dot(main_t, full[tile, cols]) + dot(rem_t[j], full[tile, BODY])).astype(BF)
-        part = share[tile, :]
+        part = shares[tile, :]
         head = part.astype(BF).astype(F32)
         pair = jnp.where(lane == spot, head, jnp.where(lane == spot + 1, part - head, 0.0))
         ends = full[tile, MAIN + CHUNK :].astype(F32)
@@ -453,7 +462,13 @@
         for k, value in enumerate((one, two)):
             cols = slice(3 * CHUNK + 128 * k, 3 * CHUNK + 128 * (k + 1))
             msg_wt[wide, cols] = (dot(main_t, full[tile, cols]) + dot(last_t, value.astype(BF))).astype(BF)
-        puts.append(put(5 + i, msg_wt.at[wide], packed_out.at[wide]))
+        put(5 + i, msg_wt.at[wide], packed_out.at[wide])
+
+    @pl.loop(0, tiles)
+    def _(i):
+        wide = tile_of(i, WIDE)
+        pltpu.make_async_copy(msg_wt.at[wide], packed_out.at[wide], leave.at[5 + i]).wait()
+
     for copy in puts:
         copy.wait()
 
@@ -475,6 +490,7 @@
             *[pltpu.VMEM(thin, BF)] * 3,
             *[pltpu.VMEM(thin, F32)] * 2,
             pltpu.VMEM((rows, MAIN + CHUNK + 128), BF),
+            pltpu.VMEM((rows, 128), F32),
             pltpu.SemaphoreType.DMA((5,)),
             pltpu.SemaphoreType.DMA((5 + rows // TILE,)),
         ],
@@ -483,7 +499,9 @@
     )(rows_msg, wt_msg, gate_w, up_w, down_w)
 
 
-def combine_kernel(copies, expert_ref, slot_ref, prob_ref, back_ref, in_ref, prob_out_ref):
+def combine_kernel(copies, expert_ref, slot_ref, slot_t_ref, prob_t_ref, back_hbm, in_ref, prob_out_ref, back_ref, sem):
+    arrive = pltpu.make_async_copy(back_hbm, back_ref, sem)
+    arrive.start()
     toks = in_ref.shape[0]
     total = back_ref.shape[0]
     col = iota((toks, total), 1)
@@ -494,7 +512,6 @@
     main, rem = zero, [zero] * 3
     sums = []
     lane = iota((toks, 128), 1)
-    first, shares = back_ref[:, 3 * CHUNK : 3 * CHUNK + 128], back_ref[:, 3 * CHUNK + 128 :]
     for k in range(expert_ref.shape[1]):
         expert, slot = expert_ref[:, k : k + 1], slot_ref[:, k : k + 1]
         kept = slot >= 0
@@ -505,23 +522,26 @@
         tail = mine & (place == CAP + high)
         for j in range(3):
             rem[j] = jnp.where(tail & (which == j), 1.0, rem[j])
-        got = dot(jnp.where(tail, 1.0, 0.0).astype(BF), shares)
-        spot = ENDS + 2 * which
-        got = jnp.where((lane == spot) | (lane == spot + 1), got, 0.0)
-        sums.append(jnp.sum(got, axis=1, keepdims=True))
-    in_ref[:, :MAIN] = dot(main.astype(BF), back_ref[...]).astype(BF)
+        sums.append((jnp.where(tail, 1.0, 0.0).astype(BF), ENDS + 2 * which))
+    main = main.astype(BF)
     rem = [value.astype(BF) for value in rem]
+    arrive.wait()
+    first, shares = back_ref[:, 3 * CHUNK : 3 * CHUNK + 128], back_ref[:, 3 * CHUNK + 128 :]
+    in_ref[:, :MAIN] = dot(main, back_ref[...]).astype(BF)
     part = dot(rem[0], back_ref[:, :CHUNK])
     for j in (1, 2):
         part = part + dot(rem[j], back_ref[:, j * CHUNK : (j + 1) * CHUNK])
     in_ref[:, BODY] = part.astype(BF)
     ends = dot(rem[0], first) + pltpu.roll(dot(rem[1], first), ENDS, 1) + dot(rem[2], shares)
     in_ref[:, MAIN + CHUNK :] = ends[:, :ENDS].astype(BF)
-    choice = iota(prob_ref.shape, 1)
-    total_share = jnp.zeros(prob_ref.shape, F32)
-    for k, value in enumerate(sums):
-        total_share = jnp.where(choice == k, value, total_share)
-    prob_out_ref[...] = jnp.where(slot_ref[...] >= 0, total_share / prob_ref[...], 0.0)
+    total_share = jnp.zeros((toks, 128), F32)
+    for k, (tail, spot) in enumerate(sums):
+        got = dot(tail, shares)
+        got = jnp.where((lane == spot) | (lane == spot + 1), got, 0.0)
+        total_share = jnp.where(lane == k, jnp.sum(got, axis=1, keepdims=True), total_share)
+    share_t = total_share.T[: prob_out_ref.shape[0], :]
+    rounded = prob_t_ref[...].astype(BF).astype(F32)
+    prob_out_ref[...] = jnp.where(slot_t_ref[...] >= 0, share_t / rounded, 0.0)
 
 
 def combine(expert_ids, slots, probs, back, width, copies):
@@ -529,10 +549,12 @@
         functools.partial(combine_kernel, copies),
         out_shape=(
             jax.ShapeDtypeStruct((expert_ids.shape[0], width), BF),
-            jax.ShapeDtypeStruct(probs.shape, F32),
+            jax.ShapeDtypeStruct(probs.T.shape, F32),
         ),
+        in_specs=[*[pl.BlockSpec(memory_space=pltpu.VMEM)] * 4, pl.BlockSpec(memory_space=pl.ANY)],
+        scratch_shapes=[pltpu.VMEM(back.shape, BF), pltpu.SemaphoreType.DMA],
         compiler_params=pltpu.CompilerParams(vmem_limit_bytes=40 * 2**20),
-    )(expert_ids, slots, probs, back)
+    )(expert_ids, slots, slots.T, probs.T, back)
 
 
 def body(tokens, cotangent, expert_ids, slots, probs, w_gate, w_up, w_down):
@@ -541,10 +563,7 @@
     devices = experts * copies
     width = tokens.shape[1]
     gate_w, up_w, down_w = w_gate[0].T, w_up[0].T, w_down[0].T
-    rounded = probs.astype(BF).astype(F32)
-    code = jnp.where(slots >= 0, expert_ids * MROWS + slots, -1).T
-    rows_msg = pack(code, tokens.T, experts)
-    table = jnp.concatenate([code.astype(F32), rounded.T], axis=0)
+    rows_msg, table = pack(expert_ids.T, slots.T, probs.T, tokens.T, experts)
     rows_in, wt_in = exchange(table, rows_msg, cotangent.T)
     rows_in = rows_in.reshape(devices * MROWS, MAIN)
     wt_in = wt_in.reshape(devices * MROWS, MAIN)
@@ -556,8 +575,8 @@
     grad_down = lax.dot_general(weighted, hidden, contract_rows, preferred_element_type=F32).astype(BF)
     grad_gate = lax.dot_general(rows, gate_grad, contract_rows, preferred_element_type=F32).astype(BF)
     grad_up = lax.dot_general(rows, up_grad, contract_rows, preferred_element_type=F32).astype(BF)
-    input_grad, prob_grad = combine(expert_ids, slots, rounded, back, width, copies)
-    return input_grad, prob_grad, grad_gate[None], grad_up[None], grad_down[None]
+    input_grad, prob_grad = combine(expert_ids, slots, probs, back, width, copies)
+    return input_grad, prob_grad.T, grad_gate[None], grad_up[None], grad_down[None]
 
 
 def solution(mesh):

time: 200 us -> 196 us (0.980)
  local copies, waits for them, and re-layouts: 4.73 us -> 1.43 us
  other arithmetic: 2.02 us -> 0.01 us
    unnamed x24 -> x21, local copies, waits for them, and re-layouts: 4.54 us -> 1.43 us
    pallas_call x1, Pallas kernels: 1.51 us -> 4.04 us  [pack(): pl.pallas_call(pack_kernel, out_shape=(jax.ShapeDtypeStruct((experts * MR...]
where the time goes in v5:
time: 196 us
  Pallas kernels  130 us (66%)
  waiting for transfers between devices  35.9 us (18%)
  matrix products  18.3 us (9%)
  starting transfers between devices  9.62 us (5%)
    pallas_call x1, Pallas kernels, exchange(): pl.pallas_call(exchange_kernel, in_specs=[anywhere] * 3, out_specs=[anywh...  84.9 us
    all_to_all x1, waiting for transfers between devices, body(): lax.all_to_all(packed.reshape(devices, MROWS, MAIN), ('expert', 'dp'), sp...  35.9 us
    pallas_call x1, Pallas kernels, expert(): pl.pallas_call(expert_kernel, in_specs=[anywhere] * 5, out_specs=[anywher...  35.8 us
    all_to_all x1, starting transfers between devices, body(): lax.all_to_all(packed.reshape(devices, MROWS, MAIN), ('expert', 'dp'), sp...  9.62 us
    dot_general x1, matrix products, body(): lax.dot_general(rows, up_grad, contract_rows, preferred_element_type=F32)  7.85 us
    pallas_call x1, Pallas kernels, combine(): pl.pallas_call(functools.partial(combine_kernel, copies), out_shape=(jax....  5.39 us
    dot_general x1, matrix products, body(): lax.dot_general(weighted, hidden, contract_rows, preferred_element_type=F32)  5.23 us
    dot_general x1, matrix products, body(): lax.dot_general(rows, gate_grad, contract_rows, preferred_element_type=F32)  5.23 us
  transfers between devices with their start and end apart: 1, of which 1 were waited for; matrix products, arithmetic and copies ran while one was open for 9% of the time, Pallas kernels for 0%

profile of v5, /device:TPU:0, one launch (start us, length us, event | category | flops | bytes accessed | tf_op | source)
XLA Modules:
  0.0 196.1 jit_solution(760502632037232832)
XLA Ops:
  0.6 4.0 %shard_map.119 = (bf16[512,2176]{1,0:T(8,128)(2,1)}, f32[8,128]{1,0:T(8,128)}) custom-call(s32[4,128]{1,0:T(4,128)} %bitcast.40, s32[4,128]{1,0:T(4,128)} %bitcast.32, f32[4,128]{1,0:T(4,128)} %bitcast.34, bf16[2880,128]{1,0:T(8,128)(2,1)} %bitcast.38), custom_call_target="tpu_custom_call" | custom-call | tf_op jit(solution)/shard_map/pallas_call | solution.py:79
  4.7 84.9 %shard_map.120 = (bf16[4,4,8,8,2176]{4,3,2,1,0:T(8,128)(2,1)}, bf16[4,4,8,8,2176]{4,3,2,1,0:T(8,128)(2,1)}) custom-call(f32[8,128]{1,0:T(8,128)} %get-tuple-element.17.table_ref, bf16[4,4,4,8,2176]{4,3,2,1,0:T(8,128)(2,1)} %bitcast.37, bf16[2880,128]{1,0:T(8,128)(2,1)} %bitcast.39), custom_call_target="tpu_custom_call" | custom-call | tf_op jit(solution)/shard_map/pallas_call | solution.py:327
  89.6 35.8 %shard_map.121 = (bf16[768,2880]{1,0:T(8,128)(2,1)}, bf16[768,2880]{1,0:T(8,128)(2,1)}, bf16[768,720]{1,0:T(8,128)(2,1)}, bf16[768,720]{1,0:T(8,128)(2,1)}, bf16...) custom-call(bf16[1024,2176]{1,0:T(8,128)(2,1)} %bitcast.41, bf16[1024,2176]{1,0:T(8,128)(2,1)} %bitcast.42, ...), custom_call_target="tpu_custom_call" | custom-call | flops 15925248000 | bytes 41943040 | tf_op jit(solution)/shard_map/pallas_call | solution.py:481
  125.3 0.0 copy-start.2
  125.3 0.0 copy-start
  125.4 0.0 copy-start.6
  125.4 9.6 %all-to-all-start = ((bf16[128,8,2176]{2,1,0:T(8,128)(2,1)}), bf16[128,8,2176]{2,1,0:T(8,128)(2,1)}, u32[]{:S(2)}, u32[]{:S(2)}) async-start(bf16[128,8,2176]{2,1,0:T(8,128)(2,1)} %bitcast.36), calls=%async_computation | async-start | bytes 8912896 | tf_op jit(solution)/shard_map/all_to_all | solution.py:571
  135.0 0.0 copy-done.2
  135.0 0.1 copy.13.expert_ref
  135.1 0.0 copy-done
  135.1 0.1 copy.14.slot_ref
  135.3 0.0 copy-start.5
  135.3 0.0 slice-start
  135.3 7.8 %fusion.1 = bf16[1,2880,720]{1,2,0:T(8,128)(2,1)} fusion(bf16[768,2880]{1,0:T(8,128)(2,1)} %get-tuple-element.24, bf16[768,720]{1,0:T(8,128)(2,1)S(1)} %copy-done.6), kind=kOutput, calls=%fused_computation.4 | convolution fusion | flops 3187123200 | bytes 9676800 | tf_op jit(solution)/shard_map/dot_general | solution.py:577
  143.1 0.0 copy-done.5
  143.1 0.0 copy-start.4
  143.1 5.2 %fusion = bf16[1,2880,720]{1,2,0:T(8,128)(2,1)} fusion(bf16[768,2880]{1,0:T(8,128)(2,1)S(1)} %copy-done.3, bf16[768,720]{1,0:T(8,128)(2,1)S(1)} %copy-done.5), kind=kOutput, calls=%fused_computation.3 | convolution fusion | flops 3187123200 | bytes 9676800 | tf_op jit(solution)/shard_map/dot_general | solution.py:576
  148.4 0.0 slice-done.1
  148.4 0.0 copy-start.1
  148.4 5.2 %fusion.2 = bf16[1,2880,720]{1,2,0:T(8,128)(2,1)} fusion(bf16[768,2880]{1,0:T(8,128)(2,1)S(1)} %bitcast.48, bf16[768,720]{1,0:T(8,128)(2,1)S(1)} %copy-done.4), kind=kOutput, calls=%fused_computation.5 | convolution fusion | flops 3187123200 | bytes 9676800 | tf_op jit(solution)/shard_map/dot_general | solution.py:575
  153.6 35.9 %all-to-all-done = bf16[128,8,2176]{2,1,0:T(8,128)(2,1)} async-done(((bf16[128,8,2176]{2,1,0:T(8,128)(2,1)}), bf16[128,8,2176]{2,1,0:T(8,128)(2,1)}, u32[]{:S(2)}, u32[]{:S(2)}) %all-to-all-start) | async-done | bytes 4456480 | tf_op jit(solution)/shard_map/all_to_all | solution.py:571
  189.6 0.0 copy-done.1
  189.6 5.4 %shard_map.122 = (bf16[128,2880]{1,0:T(8,128)(2,1)S(1)}, f32[4,128]{1,0:T(4,128)}) custom-call(s32[128,4]{1,0:T(8,128)S(1)} %copy.13.expert_ref, s32[128,4]{1,0:T(8,128)S(1)} %copy.14.slot_ref, s32[4,128]{1,0:T(4,128)S(1)} %bitcast.33, f32[4,128]{1,0:T(4,128)S(1)} %bitcast.35, bf16[1024,2176]{1,0:T(8,128)(2,1)} %bitcast.15.back_hbm), custom_call_target="tpu_custom_call" | custom-call | tf_op jit(solution)/shard_map/pallas_call | solution.py:548
  195.0 1.2 copy.15
  (7 shorter events, 0.0 us)
Async XLA Ops:
  125.3 9.7 %copy-start.2 = (s32[128,4]{0,1:T(4,128)S(1)}, s32[128,4]{0,1:T(4,128)}, u32[]{:S(2)}) copy-start(s32[128,4]{0,1:T(4,128)} %param.10) | copy-start | bytes 6148
  125.3 9.8 %copy-start = (s32[128,4]{0,1:T(4,128)S(1)}, s32[128,4]{0,1:T(4,128)}, u32[]{:S(2)}) copy-start(s32[128,4]{0,1:T(4,128)} %param.11) | copy-start | bytes 6148
  125.4 9.9 %copy-start.6 = (bf16[768,720]{1,0:T(8,128)(2,1)S(1)}, bf16[768,720]{1,0:T(8,128)(2,1)}, u32[]{:S(2)}) copy-start(bf16[768,720]{1,0:T(8,128)(2,1)} %get-tuple-element.26) | copy-start | bytes 3317764
  125.4 64.2 %all-to-all-start = ((bf16[128,8,2176]{2,1,0:T(8,128)(2,1)}), bf16[128,8,2176]{2,1,0:T(8,128)(2,1)}, u32[]{:S(2)}, u32[]{:S(2)}) async-start(bf16[128,8,2176]{2,1,0:T(8,128)(2,1)} %bitcast.36), calls=%async_computation | async-start | bytes 8912896 | tf_op jit(solution)/shard_map/all_to_all | solution.py:571
  135.2 7.9 %copy-start.3 = (bf16[768,2880]{1,0:T(8,128)(2,1)S(1)}, bf16[768,2880]{1,0:T(8,128)(2,1)}, u32[]{:S(2)}) copy-start(bf16[768,2880]{1,0:T(8,128)(2,1)} %get-tuple-element.24) | copy-start | bytes 13271044
  135.3 7.9 %copy-start.5 = (bf16[768,720]{1,0:T(8,128)(2,1)S(1)}, bf16[768,720]{1,0:T(8,128)(2,1)}, u32[]{:S(2)}) copy-start(bf16[768,720]{1,0:T(8,128)(2,1)} %get-tuple-element.25) | copy-start | bytes 3317764
  135.3 13.1 %slice-start = ((s8[4521984]{0:T(1024)(128)(4,1)}), s8[4194304]{0:T(1024)(128)(4,1)S(1)}, s32[]{:S(2)}) async-start(s8[4521984]{0:T(1024)(128)(4,1)} %bitcast.47), calls=%async_computation.1 | async-start | bytes 8388608
  143.1 5.3 %slice-start.1 = ((s8[4521984]{0:T(1024)(128)(4,1)}), s8[327680]{0:T(1024)(128)(4,1)S(1)}, s32[]{:S(2)}) async-start(s8[4521984]{0:T(1024)(128)(4,1)} %bitcast.47), calls=%async_computation.2 | async-start | bytes 655360
  143.1 5.3 %copy-start.4 = (bf16[768,720]{1,0:T(8,128)(2,1)S(1)}, bf16[768,720]{1,0:T(8,128)(2,1)}, u32[]{:S(2)}) copy-start(bf16[768,720]{1,0:T(8,128)(2,1)} %get-tuple-element.28) | copy-start | bytes 3317764
  148.4 41.2 %copy-start.1 = (f32[128,4]{0,1:T(4,128)S(1)}, f32[128,4]{0,1:T(4,128)}, u32[]{:S(2)}) copy-start(f32[128,4]{0,1:T(4,128)} %param.12) | copy-start | bytes 6148

commit v6 on v5

--- a/solution.py
+++ b/solution.py
@@ -29,6 +29,51 @@
 
 def iota(shape, dim):
     return lax.broadcasted_iota(jnp.int32, shape, dim)
+
+
+TILE = 192
+WIDE = TILE // CAP * MROWS
+
+
+def tile_of(i, size):
+    return pl.ds(pl.multiple_of(i * size, size), size)
+
+
+def picks(out_rows, in_rows, wide, reorder=False):
+    if wide:
+        q, o = iota((out_rows, in_rows), 0), iota((out_rows, in_rows), 1)
+    else:
+        o, q = iota((out_rows, in_rows), 0), iota((out_rows, in_rows), 1)
+    message = o // CAP
+    slot = o - CAP * message
+    if reorder:
+        at = message % 8
+        base = q - MROWS * (message - at + (at % 4) * 2 + at // 4)
+    else:
+        base = q - MROWS * message
+    high = jnp.where(slot >= 3, 1, 0)
+    main = jnp.where(base == slot, 1.0, 0.0).astype(BF)
+    last = base == CAP + high
+    rem = [jnp.where(last & (slot - 3 * high == j), 1.0, 0.0).astype(BF) for j in range(3)]
+    return main, rem, jnp.where(last, 1.0, 0.0).astype(BF)
+
+
+def unpack(src, dst, start, stop):
+    main, rem, _ = picks(TILE, WIDE, False)
+
+    @pl.loop(0, dst.shape[0] // TILE)
+    def _(i):
+        wide, tile = tile_of(i, WIDE), tile_of(i, TILE)
+        dst[tile, start:stop] = dot(main, src[wide, start:stop]).astype(BF)
+        if stop < MAIN:
+            return
+        part = dot(rem[0], src[wide, :CHUNK])
+        for j in (1, 2):
+            part = part + dot(rem[j], src[wide, j * CHUNK : (j + 1) * CHUNK])
+        dst[tile, BODY] = part.astype(BF)
+        one, two = src[wide, 3 * CHUNK : 3 * CHUNK + 128], src[wide, 3 * CHUNK + 128 :]
+        ends = dot(rem[0], one) + pltpu.roll(dot(rem[1], one), ENDS, 1) + dot(rem[2], two)
+        dst[tile, MAIN + CHUNK :] = ends[:, :ENDS].astype(BF)
 
 
 def pack_kernel(expert_ref, slot_ref, prob_ref, tok_ref, rows_ref, table_ref, rem_ref):
@@ -95,10 +140,11 @@
 EARLY = True
 
 
-def exchange_kernel(table_ref, rows_ref, cot_ref, rows_out, wt_out, *scratch):
+def exchange_kernel(table_ref, rows_ref, cot_ref, gate_hbm, up_hbm, wt_out, full_out, hidden_out, glu_out, slope_out, *scratch):
     relay_a, held_a, relay_b = scratch[:2], scratch[2:4], scratch[4:6]
     (cots, tables, sent, rest, block_buf) = scratch[6:11]
-    (tab_s, tab_r, cot_s, cot_r, a1_s, a1_r, a2_s, a2_r, a3_s, a3_r, b1_s, b1_r, b2_s, b2_r, own) = scratch[11:]
+    (rows_out, gate_w, up_w, full_rows, hidden, glu, slope) = scratch[11:18]
+    (tab_s, tab_r, cot_s, cot_r, a1_s, a1_r, a2_s, a2_r, a3_s, a3_r, b1_s, b1_r, b2_s, b2_r, own) = scratch[18:]
     e, d = lax.axis_index("expert"), lax.axis_index("dp")
     z, y, x, c = e // 16, (e // 4) % 4, d * 2 + (e // 2) % 2, e % 2
     xc, sub = x * 2 + c, (x % 2) * 2 + c
@@ -197,18 +243,20 @@
             a1[h][i].wait_recv()
             forward_rows(h, i, (mine[h] - STEPS[i]) % 4)
 
+    line_copies, own_lines = ([], []), ([], [])
+
     def spread_rows(h, group, source, place):
         where = pick(rows_out, h, every, place, xc, every, halves[h])
         for k, off in enumerate(LINE):
             ox, oc = (x + off[0]) % 4, (c + off[1]) % 2
-            send(
+            line_copies[h].append(send(
                 source.at[:, (ox % 2) * 2 + oc],
                 where,
                 a3_s.at[h, group, k],
                 a3_r.at[h, group, k],
                 device(0, 0, *off),
-            )
-        keep(source.at[:, sub], where, own.at[4 + 4 * h + group])
+            ))
+        own_lines[h].append(keep(source.at[:, sub], where, own.at[4 + 4 * h + group]))
 
     row = iota((16 * MROWS, 1), 0)
 
@@ -275,6 +323,9 @@
         send_part(0)
     forward_a1(0)
     forward_a1(1)
+    weights = [pltpu.make_async_copy(gate_hbm, gate_w, own.at[44]), pltpu.make_async_copy(up_hbm, up_w, own.at[45])]
+    for copy in weights:
+        copy.start()
     far = []
     for i, step in enumerate((1, 3)):
         block = ((x - step) % 4) * 2 + c
@@ -298,8 +349,8 @@
     send_part(3)
     if EARLY:
         relay_part(0)
-    for j, step in enumerate(STEPS):
-        for h in range(2):
+    for h in range(2):
+        for j, step in enumerate(STEPS):
             for i in range(4):
                 a2[h][i][j].wait_recv()
             place = (mine[1 - h] - step) % 4
@@ -307,115 +358,27 @@
     for p in range(1 if EARLY else 0, 4):
         relay_part(p)
 
-    early = {id(copy) for copy in tab_copies + near + far + other_core}
-    for group in a1 + [v for half in a2 for v in half] + [v for part in b1 for v in part]:
-        early |= {id(copy) for copy in group}
-    for copy in local[4:]:
+    flat = rows_out.reshape(16 * 8 * MROWS, MAIN)
+    for copy in weights:
         copy.wait()
-    for copy in started:
-        if id(copy) not in early:
-            copy.wait_recv()
-    for copy in started:
-        copy.wait_send()
-
-
-def exchange(table, rows_msg, cot_t):
-    out = jax.ShapeDtypeStruct((4, 4, 8, MROWS, MAIN), BF)
-    anywhere = pl.BlockSpec(memory_space=pl.ANY)
-    shapes = [(7,), (9,), (2, 3), (2, 4, 3), (2, 4, 7), (PARTS, 2, 3), (PARTS, 2, 4, 3)]
-    sems = [pltpu.SemaphoreType.DMA(shape) for shape in shapes for _ in range(2)]
-    return pl.pallas_call(
-        exchange_kernel,
-        in_specs=[anywhere] * 3,
-        out_specs=[anywhere] * 2,
-        out_shape=[out, out],
-        scratch_shapes=[
-            *[pltpu.VMEM((4, 4, at, MROWS, half), BF) for at in (4, 4, 8) for half in WIDTHS],
-            pltpu.VMEM((8, *cot_t.shape), BF),
-            pltpu.VMEM((8, *table.shape), F32),
-            pltpu.VMEM((4, 4, 8, MROWS, MAIN), BF),
-            pltpu.VMEM((MAIN - 3 * CHUNK, 3 * cot_t.shape[1]), BF),
-            pltpu.VMEM((16 * MROWS, MAIN), BF),
-            *sems,
-            pltpu.SemaphoreType.DMA((12 + 8 * PARTS,)),
-        ],
-        compiler_params=pltpu.CompilerParams(collective_id=0, has_side_effects=True, vmem_limit_bytes=67_043_328),
-    )(table, rows_msg.reshape(4, 4, 4, MROWS, MAIN), cot_t)
-
-
-def picks(out_rows, in_rows, wide, reorder=False):
-    if wide:
-        q, o = iota((out_rows, in_rows), 0), iota((out_rows, in_rows), 1)
-    else:
-        o, q = iota((out_rows, in_rows), 0), iota((out_rows, in_rows), 1)
-    message = o // CAP
-    slot = o - CAP * message
-    if reorder:
-        at = message % 8
-        base = q - MROWS * (message - at + (at % 4) * 2 + at // 4)
-    else:
-        base = q - MROWS * message
-    high = jnp.where(slot >= 3, 1, 0)
-    main = jnp.where(base == slot, 1.0, 0.0).astype(BF)
-    last = base == CAP + high
-    rem = [jnp.where(last & (slot - 3 * high == j), 1.0, 0.0).astype(BF) for j in range(3)]
-    return main, rem, jnp.where(last, 1.0, 0.0).astype(BF)
-
-
-TILE = 192
-WIDE = TILE // CAP * MROWS
-
-
-def expert_kernel(rows_msg, wt_msg, gate_hbm, up_hbm, down_hbm, *refs):
-    outs, bufs, sems = refs[:6], refs[6:-2], refs[-2:]
-    msg_rows, msg_wt, gate_w, up_w, down_w, rows, weighted, hidden, gate_grad, up_grad, glu, slope, full, shares = bufs
-    rows_out, weighted_out, hidden_out, gate_grad_out, up_grad_out, packed_out = outs
-    arrive, leave = sems
-    total, width = rows.shape
-    tiles = total // TILE
-
-    def tile_of(i, size):
-        return pl.ds(pl.multiple_of(i * size, size), size)
-
-    def fetch(i, src, dst):
-        copy = pltpu.make_async_copy(src, dst, arrive.at[i])
-        copy.start()
-        return copy
-
-    def put(i, src, dst):
-        copy = pltpu.make_async_copy(src, dst, leave.at[i])
-        copy.start()
-        return copy
-
-    got_rows = fetch(0, rows_msg, msg_rows)
-    got_gate = fetch(1, gate_hbm, gate_w)
-    got_up = fetch(2, up_hbm, up_w)
-    got_wt = fetch(3, wt_msg, msg_wt)
-    got_down = fetch(4, down_hbm, down_w)
-    main, rem, _ = picks(TILE, WIDE, False)
-
-    def unpack(src, dst):
-        @pl.loop(0, tiles)
-        def _(i):
-            wide, tile = tile_of(i, WIDE), tile_of(i, TILE)
-            dst[tile, :MAIN] = dot(main, src[wide, :MAIN]).astype(BF)
-            part = dot(rem[0], src[wide, :CHUNK])
-            for j in (1, 2):
-                part = part + dot(rem[j], src[wide, j * CHUNK : (j + 1) * CHUNK])
-            dst[tile, BODY] = part.astype(BF)
-            one, two = src[wide, 3 * CHUNK : 3 * CHUNK + 128], src[wide, 3 * CHUNK + 128 :]
-            ends = dot(rem[0], one) + pltpu.roll(dot(rem[1], one), ENDS, 1) + dot(rem[2], two)
-            dst[tile, MAIN + CHUNK :] = ends[:, :ENDS].astype(BF)
-
-    got_rows.wait()
-    unpack(msg_rows, rows)
-    puts = [put(0, rows, rows_out)]
-    got_gate.wait()
-    glu[...] = dot_nt(rows[...], gate_w[...])
-    got_up.wait()
-    slope[...] = dot_nt(rows[...], up_w[...])
-
-    @pl.loop(0, tiles)
+    cut = WIDTHS[0]
+    for copy in own_lines[0]:
+        copy.wait()
+    for copy in line_copies[0]:
+        copy.wait_recv()
+    unpack(flat, full_rows, 0, cut)
+    glu[...] = dot_nt(full_rows[:, :cut], gate_w[:, :cut])
+    slope[...] = dot_nt(full_rows[:, :cut], up_w[:, :cut])
+    for copy in own_lines[1]:
+        copy.wait()
+    for copy in line_copies[1]:
+        copy.wait_recv()
+    unpack(flat, full_rows, cut, MAIN)
+    keep(full_rows, full_out, own.at[46])
+    glu[...] += dot_nt(full_rows[:, cut:], gate_w[:, cut:])
+    slope[...] += dot_nt(full_rows[:, cut:], up_w[:, cut:])
+
+    @pl.loop(0, full_rows.shape[0] // TILE)
     def _(i):
         tile = tile_of(i, TILE)
         gate, up = glu[tile, :], slope[tile, :] + 1.0
@@ -425,11 +388,87 @@
         glu[tile, :] = prod
         slope[tile, :] = up * (sig + ALPHA * prod * (1.0 - sig))
 
-    puts.append(put(1, hidden, hidden_out))
-    got_wt.wait()
-    unpack(msg_wt, weighted)
+    for i, (src, dst) in enumerate(((hidden, hidden_out), (glu, glu_out), (slope, slope_out))):
+        keep(src, dst, own.at[47 + i])
+    early = {id(copy) for copy in tab_copies + near + far + other_core}
+    for group in a1 + [v for half in a2 for v in half] + [v for part in b1 for v in part]:
+        early |= {id(copy) for copy in group}
+    for half in line_copies + own_lines:
+        early |= {id(copy) for copy in half}
+    for copy in local[4:]:
+        if id(copy) not in early:
+            copy.wait()
+    for copy in started:
+        if id(copy) not in early:
+            copy.wait_recv()
+    for copy in started:
+        copy.wait_send()
+
+
+def exchange(table, rows_msg, cot_t, gate_w, up_w):
+    out = jax.ShapeDtypeStruct((4, 4, 8, MROWS, MAIN), BF)
+    units, width = gate_w.shape
+    rows = 16 * 8 * CAP
+    anywhere = pl.BlockSpec(memory_space=pl.ANY)
+    shapes = [(7,), (9,), (2, 3), (2, 4, 3), (2, 4, 7), (PARTS, 2, 3), (PARTS, 2, 4, 3)]
+    sems = [pltpu.SemaphoreType.DMA(shape) for shape in shapes for _ in range(2)]
+    return pl.pallas_call(
+        exchange_kernel,
+        in_specs=[anywhere] * 5,
+        out_specs=[anywhere] * 5,
+        out_shape=[
+            out,
+            jax.ShapeDtypeStruct((rows, width), BF),
+            jax.ShapeDtypeStruct((rows, units), BF),
+            jax.ShapeDtypeStruct((rows, units), F32),
+            jax.ShapeDtypeStruct((rows, units), F32),
+        ],
+        scratch_shapes=[
+            *[pltpu.VMEM((4, 4, at, MROWS, half), BF) for at in (4, 4, 8) for half in WIDTHS],
+            pltpu.VMEM((8, *cot_t.shape), BF),
+            pltpu.VMEM((8, *table.shape), F32),
+            pltpu.VMEM((4, 4, 8, MROWS, MAIN), BF),
+            pltpu.VMEM((MAIN - 3 * CHUNK, 3 * cot_t.shape[1]), BF),
+            pltpu.VMEM((16 * MROWS, MAIN), BF),
+            pltpu.VMEM((4, 4, 8, MROWS, MAIN), BF),
+            pltpu.VMEM((units, width), BF),
+            pltpu.VMEM((units, width), BF),
+            pltpu.VMEM((rows, width), BF),
+            pltpu.VMEM((rows, units), BF),
+            pltpu.VMEM((rows, units), F32),
+            pltpu.VMEM((rows, units), F32),
+            *sems,
+            pltpu.SemaphoreType.DMA((50,)),
+        ],
+        compiler_params=pltpu.CompilerParams(collective_id=0, has_side_effects=True, vmem_limit_bytes=67_043_328),
+    )(table, rows_msg.reshape(4, 4, 4, MROWS, MAIN), cot_t, gate_w, up_w)
+
+
+def expert_kernel(wt_msg, hidden_hbm, glu_hbm, slope_hbm, gate_hbm, up_hbm, down_hbm, *refs):
+    outs, bufs, sems = refs[:4], refs[4:-2], refs[-2:]
+    msg_wt, hidden, glu, slope, gate_w, up_w, down_w, weighted, gate_grad, up_grad, full, shares = bufs
+    weighted_out, gate_grad_out, up_grad_out, packed_out = outs
+    arrive, leave = sems
+    total, width = weighted.shape
+    tiles = total // TILE
+    fetched = []
+    for src, dst in (
+        (wt_msg, msg_wt), (down_hbm, down_w), (hidden_hbm, hidden), (glu_hbm, glu), (slope_hbm, slope), (gate_hbm, gate_w), (up_hbm, up_w)
+    ):
+        fetched.append(pltpu.make_async_copy(src, dst, arrive.at[len(fetched)]))
+        fetched[-1].start()
+    puts = []
+
+    def put(i, src, dst):
+        copy = pltpu.make_async_copy(src, dst, leave.at[i])
+        copy.start()
+        return copy
+
+    fetched[0].wait()
+    unpack(msg_wt, weighted, 0, MAIN)
     puts.append(put(2, weighted, weighted_out))
-    got_down.wait()
+    for copy in fetched[1:5]:
+        copy.wait()
     main_t, rem_t, last_t = picks(WIDE, TILE, True, True)
     lane = iota((TILE, 128), 1)
     slot = iota((TILE, 128), 0) % CAP
@@ -441,6 +480,8 @@
     gate_grad[...] = (hgrad * slope[...]).astype(BF)
     puts.append(put(3, gate_grad, gate_grad_out))
     puts.append(put(4, up_grad, up_grad_out))
+    for copy in fetched[5:]:
+        copy.wait()
     full[:, width:] = jnp.zeros((total, full.shape[1] - width), BF)
     for start in range(0, width, 768):
         cols = slice(start, min(width, start + 768))
@@ -473,30 +514,31 @@
         copy.wait()
 
 
-def expert(rows_msg, wt_msg, gate_w, up_w, down_w):
+def expert(wt_msg, hidden, glu, slope, gate_w, up_w, down_w):
     units, width = gate_w.shape
-    rows = rows_msg.shape[0] // MROWS * CAP
+    rows = hidden.shape[0]
     anywhere = pl.BlockSpec(memory_space=pl.ANY)
     wide, thin = (rows, width), (rows, units)
     return pl.pallas_call(
         expert_kernel,
-        in_specs=[anywhere] * 5,
-        out_specs=[anywhere] * 6,
-        out_shape=[jax.ShapeDtypeStruct(shape, BF) for shape in (wide, wide, thin, thin, thin, rows_msg.shape)],
+        in_specs=[anywhere] * 7,
+        out_specs=[anywhere] * 4,
+        out_shape=[jax.ShapeDtypeStruct(shape, BF) for shape in (wide, thin, thin, wt_msg.shape)],
         scratch_shapes=[
-            *[pltpu.VMEM(rows_msg.shape, BF)] * 2,
+            pltpu.VMEM(wt_msg.shape, BF),
+            pltpu.VMEM(thin, BF),
+            *[pltpu.VMEM(thin, F32)] * 2,
             *[pltpu.VMEM((units, width), BF)] * 3,
-            *[pltpu.VMEM(wide, BF)] * 2,
-            *[pltpu.VMEM(thin, BF)] * 3,
-            *[pltpu.VMEM(thin, F32)] * 2,
+            pltpu.VMEM(wide, BF),
+            *[pltpu.VMEM(thin, BF)] * 2,
             pltpu.VMEM((rows, MAIN + CHUNK + 128), BF),
             pltpu.VMEM((rows, 128), F32),
-            pltpu.SemaphoreType.DMA((5,)),
+            pltpu.SemaphoreType.DMA((7,)),
             pltpu.SemaphoreType.DMA((5 + rows // TILE,)),
         ],
         compiler_params=pltpu.CompilerParams(vmem_limit_bytes=62 * 2**20),
-        cost_estimate=pl.CostEstimate(flops=10 * rows * width * units, bytes_accessed=40 * 2**20, transcendentals=0),
-    )(rows_msg, wt_msg, gate_w, up_w, down_w)
+        cost_estimate=pl.CostEstimate(flops=6 * rows * width * units, bytes_accessed=40 * 2**20, transcendentals=0),
+    )(wt_msg, hidden, glu, slope, gate_w, up_w, down_w)
 
 
 def combine_kernel(copies, expert_ref, slot_ref, slot_t_ref, prob_t_ref, back_hbm, in_ref, prob_out_ref, back_ref, sem):
@@ -564,10 +606,9 @@
     width = tokens.shape[1]
     gate_w, up_w, down_w = w_gate[0].T, w_up[0].T, w_down[0].T
     rows_msg, table = pack(expert_ids.T, slots.T, probs.T, tokens.T, experts)
-    rows_in, wt_in = exchange(table, rows_msg, cotangent.T)
-    rows_in = rows_in.reshape(devices * MROWS, MAIN)
+    wt_in, rows, hidden, glu, slope = exchange(table, rows_msg, cotangent.T, gate_w, up_w)
     wt_in = wt_in.reshape(devices * MROWS, MAIN)
-    rows, weighted, hidden, gate_grad, up_grad, packed = expert(rows_in, wt_in, gate_w, up_w, down_w)
+    weighted, gate_grad, up_grad, packed = expert(wt_in, hidden, glu, slope, gate_w, up_w, down_w)
     back = lax.all_to_all(
         packed.reshape(devices, MROWS, MAIN), ("expert", "dp"), split_axis=0, concat_axis=0, tiled=True
     ).reshape(devices * MROWS, MAIN)

time: 196 us -> 193 us (0.985)
  Pallas kernels: 130 us -> 126 us
  matrix products: 18.3 us -> 20.9 us
  waiting for transfers between devices: 35.9 us -> 33.4 us
    pallas_call x2, Pallas kernels: 121 us -> 116 us  [the longest x1 94.1 us: exchange(): pl.pallas_call(exchange_kernel, in_specs=[anywhere] * 5, out_specs=[anywh...]
    dot_general x1, matrix products: 5.23 us -> 7.85 us  [body(): lax.dot_general(weighted, hidden, contract_rows, preferred_element_type=F32)]
    all_to_all x1, waiting for transfers between devices: 35.9 us -> 33.4 us  [body(): lax.all_to_all(packed.reshape(devices, MROWS, MAIN), ('expert', 'dp'), sp...]
  transfers between devices with their start and end apart: 1 -> 1, of which waited for: 1 -> 1; matrix products, arithmetic and copies ran while one was open for 9% -> 11% of each run, Pallas kernels for 0% -> 0%
where the time goes in v6:
time: 193 us
  Pallas kernels  126 us (65%)
  waiting for transfers between devices  33.4 us (17%)
  matrix products  20.9 us (11%)
  starting transfers between devices  10.9 us (6%)
    pallas_call x1, Pallas kernels, exchange(): pl.pallas_call(exchange_kernel, in_specs=[anywhere] * 5, out_specs=[anywh...  94.1 us
    all_to_all x1, waiting for transfers between devices, body(): lax.all_to_all(packed.reshape(devices, MROWS, MAIN), ('expert', 'dp'), sp...  33.4 us
    pallas_call x1, Pallas kernels, expert(): pl.pallas_call(expert_kernel, in_specs=[anywhere] * 7, out_specs=[anywher...  22 us
    all_to_all x1, starting transfers between devices, body(): lax.all_to_all(packed.reshape(devices, MROWS, MAIN), ('expert', 'dp'), sp...  10.9 us
    dot_general x1, matrix products, body(): lax.dot_general(weighted, hidden, contract_rows, preferred_element_type=F32)  7.85 us
    dot_general x1, matrix products, body(): lax.dot_general(rows, up_grad, contract_rows, preferred_element_type=F32)  7.79 us
    pallas_call x1, Pallas kernels, combine(): pl.pallas_call(functools.partial(combine_kernel, copies), out_shape=(jax....  5.39 us
    dot_general x1, matrix products, body(): lax.dot_general(rows, gate_grad, contract_rows, preferred_element_type=F32)  5.23 us
  transfers between devices with their start and end apart: 1, of which 1 were waited for; matrix products, arithmetic and copies ran while one was open for 11% of the time, Pallas kernels for 0%

profile of v6, /device:TPU:0, one launch (start us, length us, event | category | flops | bytes accessed | tf_op | source)
XLA Modules:
  0.0 192.9 jit_solution(16151675150168603533)
XLA Ops:
  0.6 4.0 %shard_map.119 = (bf16[512,2176]{1,0:T(8,128)(2,1)}, f32[8,128]{1,0:T(8,128)}) custom-call(s32[4,128]{1,0:T(4,128)} %bitcast.43, s32[4,128]{1,0:T(4,128)} %bitcast.31, f32[4,128]{1,0:T(4,128)} %bitcast.33, bf16[2880,128]{1,0:T(8,128)(2,1)} %bitcast.41), custom_call_target="tpu_custom_call" | custom-call | tf_op jit(solution)/shard_map/pallas_call | solution.py:124
  4.7 94.1 %shard_map.120 = (bf16[4,4,8,8,2176]{4,3,2,1,0:T(8,128)(2,1)}, bf16[768,2880]{1,0:T(8,128)(2,1)}, bf16[768,720]{1,0:T(8,128)(2,1)}, f32[768,720]{1,0:T(8,128)}, f32[768,720]{1,0:T(8,128)}) custom-call(f32[8,128]{1,0:T(8,128)} %get-tuple-element.18.table_ref, bf16[4,4,4,8,2176]{4,3,2,1,0:T(8,128)(2,1)} %bitcast.40, bf16[2880,128]{1,0:T(8,128)(2,1)} %bitcast.42, ...), custom_call_target="tpu_custom_call" | custom-call | tf_op jit(solution)/shard_map/pallas_call | solution.py:415
  98.8 22.0 %shard_map.121 = (bf16[768,2880]{1,0:T(8,128)(2,1)}, bf16[768,720]{1,0:T(8,128)(2,1)}, bf16[768,720]{1,0:T(8,128)(2,1)}, bf16[1024,2176]{1,0:T(8,128)(2,1)}) custom-call(bf16[1024,2176]{1,0:T(8,128)(2,1)} %bitcast.46, bf16[768,720]{1,0:T(8,128)(2,1)} %get-tuple-element.21.hidden_hbm, f32[768,720]{1,0:T(8,128)} %get-tuple-element.22.glu_hbm, ...), custom_call_target="tpu_custom_call" | custom-call | flops 9555148800 | bytes 41943040 | tf_op jit(solution)/shard_map/pallas_call | solution.py:522
  120.8 0.0 copy-start.2
  120.8 0.0 copy-start
  120.8 0.0 copy-start.3
  120.8 10.9 %all-to-all-start = ((bf16[128,8,2176]{2,1,0:T(8,128)(2,1)}), bf16[128,8,2176]{2,1,0:T(8,128)(2,1)}, u32[]{:S(2)}, u32[]{:S(2)}) async-start(bf16[128,8,2176]{2,1,0:T(8,128)(2,1)} %bitcast.35), calls=%async_computation | async-start | bytes 8912896 | tf_op jit(solution)/shard_map/all_to_all | solution.py:612
  131.8 0.0 copy-done.2
  131.8 0.1 copy.13.expert_ref
  131.9 0.0 copy-done
  131.9 0.1 copy.14.slot_ref
  132.0 0.0 copy-done.3
  132.0 0.0 copy-start.5
  132.0 0.0 slice-start
  132.0 7.8 %fusion.2 = bf16[1,2880,720]{1,2,0:T(8,128)(2,1)} fusion(bf16[768,2880]{1,0:T(8,128)(2,1)} %get-tuple-element.30, bf16[768,720]{1,0:T(8,128)(2,1)S(1)} %copy-done.3), kind=kOutput, calls=%fused_computation.5 | convolution fusion | flops 3187123200 | bytes 9676800 | tf_op jit(solution)/shard_map/dot_general | solution.py:616
  139.9 0.0 copy-done.5
  139.9 7.8 %fusion.1 = bf16[1,2880,720]{1,2,0:T(8,128)(2,1)} fusion(bf16[768,2880]{1,0:T(8,128)(2,1)} %get-tuple-element.27, bf16[768,720]{1,0:T(8,128)(2,1)S(1)} %copy-done.5), kind=kOutput, calls=%fused_computation.4 | convolution fusion | flops 3187123200 | bytes 9676800 | tf_op jit(solution)/shard_map/dot_general | solution.py:618
  147.7 0.0 slice-done
  147.7 0.0 slice-done.1
  147.7 0.0 copy-start.1
  147.7 5.2 %fusion = bf16[1,2880,720]{1,2,0:T(8,128)(2,1)} fusion(bf16[768,2880]{1,0:T(8,128)(2,1)S(1)} %bitcast.45, bf16[768,720]{1,0:T(8,128)(2,1)S(1)} %copy-done.4), kind=kOutput, calls=%fused_computation.3 | convolution fusion | flops 3187123200 | bytes 9676800 | tf_op jit(solution)/shard_map/dot_general | solution.py:617
  152.9 33.4 %all-to-all-done = bf16[128,8,2176]{2,1,0:T(8,128)(2,1)} async-done(((bf16[128,8,2176]{2,1,0:T(8,128)(2,1)}), bf16[128,8,2176]{2,1,0:T(8,128)(2,1)}, u32[]{:S(2)}, u32[]{:S(2)}) %all-to-all-start) | async-done | bytes 4456480 | tf_op jit(solution)/shard_map/all_to_all | solution.py:612
  186.3 5.4 %shard_map.122 = (bf16[128,2880]{1,0:T(8,128)(2,1)S(1)}, f32[4,128]{1,0:T(4,128)}) custom-call(s32[128,4]{1,0:T(8,128)S(1)} %copy.13.expert_ref, s32[128,4]{1,0:T(8,128)S(1)} %copy.14.slot_ref, s32[4,128]{1,0:T(4,128)S(1)} %bitcast.32, f32[4,128]{1,0:T(4,128)S(1)} %bitcast.34, bf16[1024,2176]{1,0:T(8,128)(2,1)} %bitcast.14.back_hbm), custom_call_target="tpu_custom_call" | custom-call | tf_op jit(solution)/shard_map/pallas_call | solution.py:590
  191.7 1.2 copy.15
  (5 shorter events, 0.0 us)
Async XLA Ops:
  120.8 10.9 %copy-start.2 = (s32[128,4]{0,1:T(4,128)S(1)}, s32[128,4]{0,1:T(4,128)}, u32[]{:S(2)}) copy-start(s32[128,4]{0,1:T(4,128)} %param.10) | copy-start | bytes 6148
  120.8 11.1 %copy-start = (s32[128,4]{0,1:T(4,128)S(1)}, s32[128,4]{0,1:T(4,128)}, u32[]{:S(2)}) copy-start(s32[128,4]{0,1:T(4,128)} %param.11) | copy-start | bytes 6148
  120.8 11.2 %copy-start.3 = (bf16[768,720]{1,0:T(8,128)(2,1)S(1)}, bf16[768,720]{1,0:T(8,128)(2,1)}, u32[]{:S(2)}) copy-start(bf16[768,720]{1,0:T(8,128)(2,1)} %get-tuple-element.21.hidden_hbm) | copy-start | bytes 3317764
  120.8 65.5 %all-to-all-start = ((bf16[128,8,2176]{2,1,0:T(8,128)(2,1)}), bf16[128,8,2176]{2,1,0:T(8,128)(2,1)}, u32[]{:S(2)}, u32[]{:S(2)}) async-start(bf16[128,8,2176]{2,1,0:T(8,128)(2,1)} %bitcast.35), calls=%async_computation | async-start | bytes 8912896 | tf_op jit(solution)/shard_map/all_to_all | solution.py:612
  132.0 7.9 %copy-start.5 = (bf16[768,720]{1,0:T(8,128)(2,1)S(1)}, bf16[768,720]{1,0:T(8,128)(2,1)}, u32[]{:S(2)}) copy-start(bf16[768,720]{1,0:T(8,128)(2,1)} %get-tuple-element.29) | copy-start | bytes 3317764
  132.0 15.7 %slice-start = ((s8[4521984]{0:T(1024)(128)(4,1)}), s8[4194304]{0:T(1024)(128)(4,1)S(1)}, s32[]{:S(2)}) async-start(s8[4521984]{0:T(1024)(128)(4,1)} %bitcast.44), calls=%async_computation.1 | async-start | bytes 8388608
  139.9 7.8 %slice-start.1 = ((s8[4521984]{0:T(1024)(128)(4,1)}), s8[327680]{0:T(1024)(128)(4,1)S(1)}, s32[]{:S(2)}) async-start(s8[4521984]{0:T(1024)(128)(4,1)} %bitcast.44), calls=%async_computation.2 | async-start | bytes 655360
  139.9 7.8 %copy-start.4 = (bf16[768,720]{1,0:T(8,128)(2,1)S(1)}, bf16[768,720]{1,0:T(8,128)(2,1)}, u32[]{:S(2)}) copy-start(bf16[768,720]{1,0:T(8,128)(2,1)} %get-tuple-element.28) | copy-start | bytes 3317764
  147.7 38.6 %copy-start.1 = (f32[128,4]{0,1:T(4,128)S(1)}, f32[128,4]{0,1:T(4,128)}, u32[]{:S(2)}) copy-start(f32[128,4]{0,1:T(4,128)} %param.12) | copy-start | bytes 6148
